TPU v7x, 32 devices: a whole 2x2x4 slice. The times are simulated.
32 devices in a mesh: req: 4 (over z), kvh: 4 (over y, core), exp: 2 (over x).
Axes of the slice: x: 2, y: 2, z: 4, core: 2. Of those that a mesh axis runs over, the one named last changes fastest.
Arguments:
- queries: bfloat16 [512, 2048], P(('req', 'exp'), 'kvh'), may hold values from -170 to 170
- keys: bfloat16 [512, 4, 64, 128], P(('req', 'exp'), 'kvh'), may hold values from -6 to 6
- values: bfloat16 [512, 4, 64, 128], P(('req', 'exp'), 'kvh'), may hold values from -6 to 6
- lengths: int32 [512], P('req'), may hold values from 2 to 64
- out_weight: bfloat16 [2048, 2048], P(('kvh', 'exp')), may hold values from -0.125 to 0.125
- residual: bfloat16 [512, 2048], P('req'), may hold values from -54 to 54
- norm_gain: float32 [2048], replicated, may hold values from 0.5 to 2
- expert_ids: int32 [512, 8], P('req'), may hold values from 0 to 7, as said below
- gate_weights: float32 [512, 8], P('req'), may hold values from 0.2 to 1
- replica_map: int32 [16], replicated, may hold values from 0 to 7, as said below
- w_gate: bfloat16 [16, 2048, 384], P(('req', 'kvh'), None, 'exp')
- w_up: bfloat16 [16, 2048, 384], P(('req', 'kvh'), None, 'exp')
- w_down: bfloat16 [16, 384, 2048], P(('req', 'kvh'), 'exp')
Outputs:
- layer_out: bfloat16 [512, 2048], P('req', ('kvh', 'exp'))
Inputs may be any that keep to these rules, and one draw needn't show every extreme that they name: `replica_map`: every one of the 8 experts is served by one or more slots; slots that serve one expert hold equal weights in w_gate, w_up and w_down. `expert_ids`: A token names 8 different experts and every expert is named by some token; among the 128 tokens of one req index no expert is named by more than 128 tokens, and in every req index some expert is named by exactly 128.
All inputs are finite; a program needn't handle non-finite values.
Results may differ from a plain program's by a relative error of at most 0.008.
Values may be sent and summed in bfloat16 or wider, within the bound.
No kernel may reach another device: no remote copies, remote signals or barrier semaphores. Data moves between devices by JAX's collectives and lax.ppermute only.
A program may use at most 64 MiB of HBM per device.

v0:
```python
import jax
import jax.numpy as jnp
from jax import lax
from jax.sharding import PartitionSpec as P


def swapped(value, axis, apart):
    mask = 2**apart
    pairs = [(source, source ^ mask) for source in range(lax.axis_size(axis))]
    return lax.ppermute(value, axis, pairs)


def expert_runner(w_gate, w_up, w_down, complete, n_kvh, n_exp, block):

    def run(received):
        full = complete(received)
        lead_a = full.shape[0]
        lead_b = full.shape[1]
        d_model = w_gate.shape[1]
        rows = full.reshape(lead_a * lead_b, d_model)
        gate = jnp.dot(rows, w_gate[0], preferred_element_type=jnp.float32)
        up = jnp.dot(rows, w_up[0], preferred_element_type=jnp.float32)
        act = (jax.nn.silu(gate) * up).astype(jnp.bfloat16)
        down = jnp.dot(act, w_down[0], preferred_element_type=jnp.float32)
        terms = down.reshape(lead_a, lead_b, n_kvh, n_exp, block)
        summed = lax.psum_scatter(
            terms.astype(jnp.bfloat16), "exp", scatter_dimension=3, tiled=True
        )
        back = summed.reshape(lead_a, lead_b, n_kvh * block)
        return lax.all_to_all(back, "req", split_axis=0, concat_axis=0, tiled=True)

    return run


def shards(
    queries,
    keys,
    values,
    lengths,
    out_weight,
    residual,
    norm_gain,
    expert_ids,
    gate_weights,
    replica_map,
    w_gate,
    w_up,
    w_down,
):
    f32 = jnp.float32
    half_rows_count = queries.shape[0]
    n_rows = lengths.shape[0]
    head_dim = keys.shape[3]
    span = keys.shape[2]
    heads_here = queries.shape[1] // head_dim
    n_kvh = lax.axis_size("kvh")
    n_exp = lax.axis_size("exp")
    n_req = lax.axis_size("req")
    side = lax.axis_index("exp")
    own_lengths = lax.dynamic_slice_in_dim(lengths, side * half_rows_count, half_rows_count, 0)
    query = queries.reshape(half_rows_count, heads_here, head_dim)
    scores = jnp.einsum(
        "rhd,rpd->rhp", query, keys[:, 0], preferred_element_type=f32
    ) * head_dim ** (-0.5)
    position = lax.broadcasted_iota(jnp.int32, (1, 1, span), 2)
    valid = position < own_lengths[:, None, None]
    scores = jnp.where(valid, scores, -1e30)
    peak = jnp.max(scores, axis=-1)
    weights = jnp.where(valid, jnp.exp(scores - peak[..., None]), 0.0)
    total = jnp.sum(weights, axis=-1)
    probs = weights / total[..., None]
    numer = jnp.einsum(
        "rhp,rpd->rhd", probs, values[:, 0].astype(f32), precision=lax.Precision.HIGHEST
    )
    attended_part = numer.astype(jnp.bfloat16).reshape(half_rows_count, heads_here * head_dim)
    attended = lax.all_gather(attended_part, "exp", axis=0, tiled=True)
    cut = out_weight.shape[0]
    own_heads = lax.dynamic_slice_in_dim(attended, side * cut, cut, 1)
    d_model = out_weight.shape[1]
    block = d_model // (n_kvh * n_exp)
    attn_block = (
        lax.psum_scatter(
            lax.dot_general(
                out_weight, own_heads, (((0,), (1,)), ((), ())), preferred_element_type=f32
            ).astype(jnp.bfloat16),
            ("kvh", "exp"),
            scatter_dimension=0,
            tiled=True,
        )
        .astype(jnp.float32)
        .T
    )
    offset = lax.axis_index(("kvh", "exp")) * block
    mixed = lax.dynamic_slice_in_dim(residual, offset, block, 1).astype(f32) + attn_block
    squares = lax.psum(jnp.sum(mixed * mixed, axis=1), ("kvh", "exp"))
    scale = lax.rsqrt(squares / d_model + 1e-06)
    gain_block = lax.dynamic_slice_in_dim(norm_gain, offset, block, 0)
    normed = (mixed * scale[:, None] * gain_block[None, :]).astype(jnp.bfloat16)
    top = expert_ids.shape[1]
    n_slots = replica_map.shape[0]
    n_experts = n_slots // 2
    capacity = min(n_rows, max(2, (3 * n_rows * top + 2 * n_experts - 1) // (2 * n_experts)))
    probs_top = gate_weights / jnp.sum(gate_weights, axis=1, keepdims=True)
    expert_range = jnp.arange(n_experts, dtype=jnp.int32)
    owned = (replica_map[:, None] == expert_range[None, :]).astype(jnp.int32)
    earlier = jnp.cumsum(owned, axis=0) - owned
    rank = jnp.sum(earlier * owned, axis=1)
    copies = jnp.sum(owned, axis=0)
    picked = (expert_ids[..., None] == expert_range).astype(jnp.int32)
    copies_pair = jnp.sum(picked * copies, axis=-1)
    turn = jnp.full((n_rows, top), lax.axis_index("req"), jnp.int32)
    which = turn % copies_pair
    match = (replica_map == expert_ids[..., None]) & (rank == which[..., None])
    slot = jnp.argmax(match, axis=-1)
    mine = slot % n_kvh == lax.axis_index("kvh")
    flat_dest = (slot // n_kvh).reshape(-1)
    flat_mine = mine.reshape(-1)
    toward = (
        (flat_dest[:, None] == jnp.arange(n_req, dtype=jnp.int32)[None, :]) & flat_mine[:, None]
    ).astype(jnp.int32)
    before = jnp.cumsum(toward, axis=0) - toward
    place = jnp.sum(before * toward, axis=1)
    n_buffer = n_req * capacity
    target = jnp.where(flat_mine, flat_dest * capacity + place, n_buffer)
    row_of = jnp.arange(n_rows * top, dtype=jnp.int32) // top
    source = jnp.full((n_buffer,), -1, jnp.int32).at[target].set(row_of, mode="drop")
    half_rows = lax.all_gather(normed.reshape(n_rows, 1, block), "kvh", axis=1, tiled=True).reshape(
        n_rows, n_kvh * block
    )

    def complete(received):
        partner = swapped(received, "exp", 0)
        lead_a = received.shape[0]
        lead_b = received.shape[1]
        own_part = received.reshape(lead_a, lead_b, n_kvh, 1, block)
        other_part = partner.reshape(lead_a, lead_b, n_kvh, 1, block)
        first = jnp.where(side == 0, own_part, other_part)
        second = jnp.where(side == 0, other_part, own_part)
        return jnp.concatenate([first, second], axis=3).reshape(lead_a, lead_b, n_kvh * 2 * block)

    runner = expert_runner(w_gate, w_up, w_down, complete, n_kvh, n_exp, block)
    taken = half_rows[jnp.maximum(source, 0)]
    returned = runner(
        lax.all_to_all(
            jnp.where(source[:, None] >= 0, taken, jnp.zeros((), jnp.bfloat16)).reshape(
                n_req, capacity, half_rows.shape[1]
            ),
            "req",
            split_axis=0,
            concat_axis=0,
            tiled=True,
        )
    )
    flat_back = returned.reshape(n_buffer, n_kvh * block)
    gathered = flat_back[jnp.minimum(target, n_buffer - 1)].reshape(n_rows, top, n_kvh * block)
    weight = jnp.where(mine, probs_top, 0.0)
    partial_value = jnp.zeros((n_rows, n_kvh * block), f32)
    for entry in range(top):
        partial_value = partial_value + weight[:, entry, None] * gathered[:, entry].astype(f32)
    moe_block = (
        lax.psum_scatter(
            partial_value.reshape(n_rows, n_kvh, block).astype(jnp.bfloat16),
            "kvh",
            scatter_dimension=1,
            tiled=True,
        )
        .astype(jnp.float32)
        .reshape(n_rows, block)
    )
    return (mixed + moe_block).astype(jnp.bfloat16)


def solution(mesh):
    in_specs = (
        P(("req", "exp"), "kvh"),
        P(("req", "exp"), "kvh", None, None),
        P(("req", "exp"), "kvh", None, None),
        P("req"),
        P(("kvh", "exp"), None),
        P("req", None),
        P(),
        P("req", None),
        P("req", None),
        P(),
        P(("req", "kvh"), None, "exp"),
        P(("req", "kvh"), None, "exp"),
        P(("req", "kvh"), "exp", None),
    )
    out_specs = P("req", ("kvh", "exp"))
    return jax.shard_map(shards, mesh=mesh, in_specs=in_specs, out_specs=out_specs, check_vma=False)
```

profile of v0, /device:TPU:0, one launch (start us, length us, event | category | flops | bytes accessed | tf_op | source)
XLA Modules:
  0.0 304.2 jit_solution(13495541514384861496)
XLA Ops:
  6.5 0.8 dynamic_slice.13
  7.4 0.9 reshape.282
  8.3 2.0 fusion.40
  10.4 2.3 convolution_convert_fusion.2
  12.6 5.9 %all_gather.6 = bf16[128,512]{1,0:T(8,128)(2,1)S(1)} all-gather(bf16[64,512]{1,0:T(8,128)(2,1)S(1)} %bitcast.133), channel_id=1, replica_groups=mesh['req'=4,'kvh'=4,'exp'=2] {'exp'}, dimensions={0}, use_global_device_ids=true | all-gather | bytes 196608 | tf_op jit(solution)/shard_map/all_gather | solution.py:76
  18.5 1.1 fusion.1
  20.2 0.7 iota_reduce_fusion
  21.6 1.1 reduce-window.6
  23.6 0.8 dynamic_slice.15
  24.4 4.3 %scatter_custom_fusion = s32[512]{0:T(512)S(1)} fusion(s32[1024]{0:T(1024)S(1)} %bitcast.138, s32[1024]{0:T(1024)S(1)} %add_select_fusion, s32[]{:T(128)} %constant.104.clone.1), kind=kCustom, calls=%fused_computation.87 | custom fusion | bytes 2052 | tf_op jit(solution)/shard_map/scatter | solution.py:126
  28.7 27.1 %reduce-scatter.6.cloned.1.call-done = bf16[256,128]{0,1:T(8,128)(2,1)} async-done(((bf16[2048,128]{0,1:T(8,128)(2,1)}), bf16[256,128]{0,1:T(8,128)(2,1)}) %reduce-scatter.6.cloned.1.call-update) | async-done | bytes 65552 | tf_op jit(solution)/shard_map/reduce_scatter | solution.py:82
  55.8 1.0 multiply_reduce_fusion
  56.7 13.3 %psum.7 = f32[128]{0:T(128)S(1)} all-reduce(f32[128]{0:T(128)S(1)} %multiply_reduce_fusion), channel_id=1, replica_groups=mesh['req'=4,'kvh'=4,'exp'=2] {'kvh','exp'}, use_global_device_ids=true, to_apply=%region_14.15 | all-reduce | flops 128 | bytes 1024 | tf_op jit(solution)/shard_map/psum | solution.py:95
  70.1 1.0 multiply_convert_fusion
  71.1 5.8 %all-gather = bf16[128,1024]{1,0:T(8,128)(2,1)S(1)} all-gather(bf16[128,256]{1,0:T(8,128)(2,1)S(1)} %multiply_convert_fusion), channel_id=2, replica_groups=mesh['req'=4,'kvh'=4,'exp'=2] {'kvh'}, dimensions={1}, use_global_device_ids=true | all-gather | bytes 327680 | tf_op jit(solution)/shard_map/all_gather | solution.py:127
  76.8 2.0 gather_fusion
  78.9 0.7 copy.132
  79.7 30.6 %all_to_all.10 = bf16[4,128,1024]{1,2,0:T(8,128)(2,1)S(1)} all-to-all(bf16[4,128,1024]{1,2,0:T(8,128)(2,1)S(1)} %broadcast_select_fusion), channel_id=1, replica_groups=mesh['req'=4,'kvh'=4,'exp'=2] {'req'}, dimensions={0} | all-to-all | bytes 2097152 | tf_op jit(solution)/shard_map/all_to_all | solution.py:144
  110.3 0.8 collective-permute-start
  111.1 3.2 %dot_general.31 = bf16[4,2,256,192]{2,1,0,3:T(2,128)(2,1)} reshape(bf16[2048,192]{0,1:T(8,128)(2,1)} %bitcast.132) | data formatting | bytes 1572864 | tf_op jit(solution)/shard_map/dot_general | solution.py:24
  114.3 20.2 %collective-permute-done = bf16[4,128,1024]{1,2,0:T(8,128)(2,1)S(1)} collective-permute-done((bf16[4,128,1024]{1,2,0:T(8,128)(2,1)S(1)}, bf16[4,128,1024]{1,2,0:T(8,128)(2,1)S(1)}, u32[]{:S(2)}, u32[]{:S(2)}) %collective-permute-start) | collective-permute-done | bytes 1048608 | tf_op jit(solution)/shard_map/ppermute | solution.py:10
  134.9 3.9 %copy.133 = bf16[4,128,4,2,256]{4,3,2,1,0:T(2,128)(2,1)} copy(bf16[4,128,4,2,256]{1,4,2,0,3:T(8,128)(2,1)S(1)} %pad_maximum_fusion) | data formatting | bytes 4194304 | tf_op jit(solution)/shard_map/concatenate | solution.py:139
  138.8 3.3 %reshape_reshape.3 = bf16[512,2048]{1,0:T(8,128)(2,1)S(1)} reshape(bf16[4,128,4,2,256]{4,3,2,1,0:T(2,128)(2,1)} %copy.133) | data formatting | bytes 4194304 | tf_op jit(solution)/shard_map/reshape;reshape | solution.py:20
  142.1 1.3 copy-done.2
  143.5 2.0 fusion.11
  145.6 2.5 fusion.2
  148.2 2.0 convolution_convert_fusion.1
  150.2 0.6 dynamic-slice
  150.8 61.1 %all-reduce.3.cloned.1.call-done = bf16[4,128,4,2,256]{4,1,3,2,0:T(8,128)(2,1)} async-done(((bf16[4,128,4,2,256]{4,1,3,2,0:T(8,128)(2,1)}), bf16[4,128,4,2,256]{4,1,3,2,0:T(8,128)(2,1)}) %all-reduce.3.cloned.1.call-update) | async-done | bytes 2097168
  212.0 1.9 constant_dynamic-slice_fusion
  213.9 1.3 copy.136
  215.2 4.6 %all-to-all-start.1 = ((bf16[4,128,1024]{1,2,0:T(8,128)(2,1)}), bf16[4,128,1024]{1,2,0:T(8,128)(2,1)S(1)}, u32[]{:S(2)}, u32[]{:S(2)}) async-start(bf16[4,128,1024]{1,2,0:T(8,128)(2,1)} %bitcast.18), calls=%async_computation.2 | async-start | bytes 2097152 | tf_op jit(solution)/shard_map/all_to_all | solution.py:30
  219.9 25.5 %all-to-all-done.1 = bf16[4,128,1024]{1,2,0:T(8,128)(2,1)S(1)} async-done(((bf16[4,128,1024]{1,2,0:T(8,128)(2,1)}), bf16[4,128,1024]{1,2,0:T(8,128)(2,1)S(1)}, u32[]{:S(2)}, u32[]{:S(2)}) %all-to-all-start.1) | async-done | bytes 1048608 | tf_op jit(solution)/shard_map/all_to_all | solution.py:30
  245.4 0.5 copy.137
  245.9 5.4 %gather_fusion.1 = bf16[1024,1024]{1,0:T(8,128)(2,1)} fusion(bf16[512,1024]{1,0:T(8,128)(2,1)S(1)} %bitcast.118, s32[1024]{0:T(1024)S(1)} %broadcast_clamp_fusion), kind=kCustom, calls=%fused_computation.1 | custom fusion | bytes 4198400 | tf_op jit(solution)/shard_map/gather | solution.py:155
  251.3 12.5 %fusion.39 = (bf16[128,1,1024]{2,1,0:T(2,128)(2,1)S(1)}, bf16[128,1,1024]{2,1,0:T(2,128)(2,1)S(1)}, bf16[128,1,1024]{2,1,0:T(2,128)(2,1)S(1)}, bf16[128,1,1024]{...) fusion(bf16[128,8,1024]{2,1,0:T(8,128)(2,1)} %bitcast.119), kind=kLoop, calls=%fused_computation.100 | loop fusion | bytes 4194304 | tf_op jit(solution)/shard_map/slice | solution.py:159
  264.4 0.4 copy.165
  265.6 1.3 copy.163
  266.9 0.9 copy.147
  267.8 1.3 copy.162
  269.1 1.0 copy.145
  270.1 1.3 copy.161
  271.4 1.0 copy.143
  272.3 1.3 copy.160
  273.6 1.0 copy.141
  275.2 2.6 add_convert_fusion
  277.8 18.3 %reduce-scatter.8.cloned.1.call-done = bf16[128,1,256]{2,0,1:T(8,128)(2,1)} async-done(((bf16[128,4,256]{2,0,1:T(8,128)(2,1)}), bf16[128,1,256]{2,0,1:T(8,128)(2,1)}) %reduce-scatter.8.cloned.1.call-update) | async-done | bytes 65552 | tf_op jit(solution)/shard_map/reduce_scatter | solution.py:161
  296.2 1.5 fusion.16
  (66 shorter events, 4.6 us)
Async XLA Ops:
  6.5 12.0 %copy-start = (bf16[256,2048]{1,0:T(8,128)(2,1)S(1)}, bf16[256,2048]{1,0:T(8,128)(2,1)}, u32[]{:S(2)}) copy-start(bf16[256,2048]{1,0:T(8,128)(2,1)} %param.17) | copy-start | bytes 3145732
  6.5 49.2 %reduce-scatter.6.cloned.1.call-start = ((), (), s32[]{:S(2)}) async-start(), calls=%async_computation.4 | async-start | bytes 589824 | tf_op jit(solution)/shard_map/reduce_scatter | solution.py:82
  10.3 9.3 %copy-start.6 = (s32[16]{0:T(128)S(1)}, s32[16]{0:T(128)}, u32[]{:S(2)}) copy-start(s32[16]{0:T(128)} %param.22) | copy-start | bytes 196
  10.3 9.6 %copy-start.5 = (s32[128,8]{0,1:T(8,128)S(1)}, s32[128,8]{0,1:T(8,128)}, u32[]{:S(2)}) copy-start(s32[128,8]{0,1:T(8,128)} %param.20) | copy-start | bytes 12292
  10.3 10.6 %copy-start.4 = (f32[128,8]{0,1:T(8,128)S(1)}, f32[128,8]{0,1:T(8,128)}, u32[]{:S(2)}) copy-start(f32[128,8]{0,1:T(8,128)} %param.21) | copy-start | bytes 12292
  19.6 192.3 %all-reduce.3.cloned.1.call-start = ((), (), s32[]{:S(2)}) async-start(), calls=%async_computation.6 | async-start | bytes 4194304
  110.3 24.3 %collective-permute-start = (bf16[4,128,1024]{1,2,0:T(8,128)(2,1)S(1)}, bf16[4,128,1024]{1,2,0:T(8,128)(2,1)S(1)}, u32[]{:S(2)}, u32[]{:S(2)}) collective-permute-start(bf16[4,128,1024]{1,2,0:T(8,128)(2,1)S(1)} %all_to_all.10), channel_id=1, source_target_pairs={{0,1},{1,0},{2,3},{3,2},{4,5},{5,4},{6,7},{7,6},{8,9},{9,8},{10,11... | collective-permute-start | bytes 3145736 | tf_op jit(solution)/shard_map/ppermute | solution.py:10
  142.1 1.4 copy-start.2
  143.5 2.1 copy-start.7
  145.5 2.6 copy-start.1
  148.1 2.1 copy-start.8
  215.2 30.2 %all-to-all-start.1 = ((bf16[4,128,1024]{1,2,0:T(8,128)(2,1)}), bf16[4,128,1024]{1,2,0:T(8,128)(2,1)S(1)}, u32[]{:S(2)}, u32[]{:S(2)}) async-start(bf16[4,128,1024]{1,2,0:T(8,128)(2,1)} %bitcast.18), calls=%async_computation.2 | async-start | bytes 2097152 | tf_op jit(solution)/shard_map/all_to_all | solution.py:30
  219.8 76.3 %reduce-scatter.8.cloned.1.call-start = ((), (), s32[]{:S(2)}) async-start(), calls=%async_computation.5 | async-start | bytes 327680 | tf_op jit(solution)/shard_map/reduce_scatter | solution.py:161
  275.2 21.0 %copy-start.3 = (bf16[256,128]{0,1:T(8,128)(2,1)S(1)}, bf16[256,128]{0,1:T(8,128)(2,1)}, u32[]{:S(2)}) copy-start(bf16[256,128]{0,1:T(8,128)(2,1)} %reduce-scatter.6.cloned.1.call-done) | copy-start | bytes 196612
Sparse Core Ops, SparseCore 0:
  19.7 35.9 reduce-scatter.5
  150.3 61.5 all-reduce.2
  278.0 18.1 reduce-scatter.7
where the time goes:
time: 305 us; the launch traced here: 304 us
  waiting for transfers between devices  152 us (50%)
  local copies, waits for them, and re-layouts  56 us (18%)
  blocking collectives  55.6 us (18%)
  between operations  13.5 us (4%)
  matrix products  12 us (4%)
  other arithmetic  9.29 us (3%)
  starting transfers between devices  5.44 us (2%)
    unnamed x4, waiting for transfers between devices  61.2 us
    all_to_all x1, blocking collectives, shards(): lax.all_to_all(jnp.where(source[:, None] >= 0, taken, jnp.zeros((), jnp.b...  30.6 us
    reduce_scatter x1, waiting for transfers between devices, shards(): lax.psum_scatter(lax.dot_general(out_weight, own_heads, (((0,), (1,)), ((...  27.1 us
    all_to_all x1, waiting for transfers between devices, run(): return lax.all_to_all(back, 'req', split_axis=0, concat_axis=0, tiled=True)  25.5 us
    ppermute x1, waiting for transfers between devices, swapped(): return lax.ppermute(value, axis, pairs)  20.2 us
    reduce_scatter x1, waiting for transfers between devices, shards(): lax.psum_scatter(partial_value.reshape(n_rows, n_kvh, block).astype(jnp.b...  18.3 us
    psum x1, blocking collectives, shards(): squares = lax.psum(jnp.sum(mixed * mixed, axis=1), ('kvh', 'exp'))  13.3 us
    slice x1, local copies, waits for them, and re-layouts, shards(): gathered[:, entry].astype(f32)  12.5 us
  transfers between devices with their start and end apart: 5, of which 5 were waited for; matrix products, arithmetic and copies ran while one was open for 4% of the time, Pallas kernels for 0%

commit v1 on v0

--- a/solution.py
+++ b/solution.py
@@ -1,6 +1,8 @@
 import jax
 import jax.numpy as jnp
 from jax import lax
+from jax.experimental import pallas as pl
+from jax.experimental.pallas import tpu as pltpu
 from jax.sharding import PartitionSpec as P
 
 
@@ -32,7 +34,7 @@
     return run
 
 
-def shards(
+def routed_shards(
     queries,
     keys,
     values,
@@ -170,6 +172,437 @@
     return (mixed + moe_block).astype(jnp.bfloat16)
 
 
+F32 = jnp.float32
+BF16 = jnp.bfloat16
+AXES = ("req", "kvh", "exp")
+STEP = 16
+
+
+def is_dense(sizes, args):
+    queries, keys, expert_ids, replica_map = args[0], args[1], args[7], args[9]
+    n_req, n_kvh, n_exp = sizes
+    top = expert_ids.shape[1]
+    span = keys.shape[2]
+    powers = all(size & (size - 1) == 0 for size in (*sizes, span, queries.shape[0]))
+    return (
+        powers
+        and n_req >= 2
+        and n_kvh >= 2
+        and n_exp == 2
+        and top == replica_map.shape[0] // 2
+        and queries.shape[0] % (2 * STEP) == 0
+    )
+
+
+def moved(value, d_req, d_kvh, d_exp):
+    n_req, n_kvh, n_exp = (lax.axis_size(axis) for axis in AXES)
+    pairs = []
+    for req in range(n_req):
+        for kvh in range(n_kvh):
+            for exp in range(n_exp):
+                source = (req * n_kvh + kvh) * n_exp + exp
+                target = ((req ^ d_req) * n_kvh + (kvh ^ d_kvh)) * n_exp + (exp ^ d_exp)
+                pairs.append((source, target))
+    return lax.ppermute(value, AXES, pairs)
+
+
+def place():
+    kvh = lax.axis_index("kvh")
+    return lax.axis_index("req"), kvh // 2, kvh % 2, lax.axis_index("exp")
+
+
+def nt_dot(left, right, **kwargs):
+    return lax.dot_general(
+        left, right, (((1,), (1,)), ((), ())), preferred_element_type=F32, **kwargs
+    )
+
+
+def nn_dot(left, right):
+    return jnp.dot(left, right, preferred_element_type=F32)
+
+
+def in_vmem(count):
+    return [pl.BlockSpec(memory_space=pltpu.VMEM)] * count
+
+
+def in_smem():
+    return pl.BlockSpec(memory_space=pltpu.SMEM)
+
+
+def called(kernel, args, outs, flops, n_smem=0, scratch=(), name=None):
+    moves = sum(arg.size * arg.dtype.itemsize for arg in (*args, *outs))
+    return pl.pallas_call(
+        kernel,
+        out_shape=tuple(outs),
+        in_specs=[in_smem()] * n_smem + in_vmem(len(args) - n_smem),
+        out_specs=tuple(in_vmem(len(outs))),
+        scratch_shapes=list(scratch),
+        cost_estimate=pl.CostEstimate(flops=flops, bytes_accessed=moves, transcendentals=0),
+        name=name,
+    )(*args)
+
+
+def like(shape, dtype):
+    return jax.ShapeDtypeStruct(shape, dtype)
+
+
+def attention_kernel(lengths, query, key, value, ids, gates, *outs):
+    blocks, shares = outs[:4], outs[4]
+    step = pl.program_id(0)
+    _, _, core, side = place()
+    n = query.shape[0]
+    span, head_dim = key.shape[2], key.shape[3]
+    heads = query.shape[1] // head_dim
+    steps = pl.num_programs(0)
+
+    @pl.when(step == 0)
+    def _():
+        probs_top = gates[...] / jnp.sum(gates[...], axis=0, keepdims=True)
+        for expert in range(shares.shape[0]):
+            shares[expert : expert + 1, :] = jnp.sum(
+                jnp.where(ids[...] == expert, probs_top, 0.0), axis=0, keepdims=True
+            )
+
+    rows = jnp.concatenate(
+        [query[:, head * head_dim : (head + 1) * head_dim] for head in range(heads)], axis=0
+    )
+    scores = nt_dot(rows, key[...].reshape(n * span, head_dim)) * head_dim ** (-0.5)
+    column = lax.broadcasted_iota(jnp.int32, (1, n * span), 1)
+    owner = lax.shift_right_logical(column, span.bit_length() - 1)
+    limit = jnp.zeros((1, n * span), jnp.int32)
+    first = (side * steps + step) * n
+    for index in range(n):
+        limit = jnp.where(owner == index, lengths[first + index], limit)
+    live = (column & (span - 1)) < limit
+    request = lax.broadcasted_iota(jnp.int32, (heads * n, 1), 0) & (n - 1)
+    valid = (request == owner) & live
+    scores = jnp.where(valid, scores, -1e30)
+    peak = jnp.max(scores, axis=1, keepdims=True)
+    weights = jnp.where(valid, jnp.exp(scores - peak), 0.0)
+    total = jnp.sum(weights, axis=1, keepdims=True)
+    high = weights.astype(BF16)
+    low = (weights - high.astype(F32)).astype(BF16)
+    held = value[...].reshape(n * span, head_dim)
+    numer = (nn_dot(high, held) + nn_dot(low, held)) / total
+    by_head = [numer[head * n : (head + 1) * n].astype(BF16) for head in range(heads)]
+    parts = heads // 2
+    lower = jnp.concatenate(by_head[:parts], axis=1)
+    upper = jnp.concatenate(by_head[parts:], axis=1)
+    near = jnp.where(side == 0, lower, upper)
+    far = jnp.where(side == 0, upper, lower)
+    half = steps // 2
+    target_core = step // half
+    spot = pl.ds(pl.multiple_of((step % half) * n, n), n)
+
+    @pl.when(target_core == core)
+    def _():
+        blocks[0][spot, :] = near
+        blocks[1][spot, :] = far
+
+    @pl.when(target_core != core)
+    def _():
+        blocks[2][spot, :] = near
+        blocks[3][spot, :] = far
+
+
+def attention(queries, keys, values, lengths, ids, gates, n_experts):
+    rows = queries.shape[0]
+    steps = rows // STEP
+    span, head_dim = keys.shape[2], keys.shape[3]
+    piece = like((rows // 2, queries.shape[1] // 2), BF16)
+    outs = [piece] * 4 + [like((n_experts, ids.shape[1]), F32)]
+    whole = lambda shape: pl.BlockSpec(shape, lambda step: (0, 0))
+    cache = pl.BlockSpec((STEP, 1, span, head_dim), lambda step: (step, 0, 0, 0))
+    return pl.pallas_call(
+        attention_kernel,
+        grid=(steps,),
+        out_shape=tuple(outs),
+        in_specs=[
+            in_smem(),
+            pl.BlockSpec((STEP, queries.shape[1]), lambda step: (step, 0)),
+            cache,
+            cache,
+            whole(ids.shape),
+            whole(gates.shape),
+        ],
+        out_specs=tuple(whole(out.shape) for out in outs),
+        cost_estimate=pl.CostEstimate(
+            flops=6 * STEP * rows * queries.shape[1] * span,
+            bytes_accessed=2 * keys.size * 2,
+            transcendentals=0,
+        ),
+        name="attention",
+    )(lengths, queries, keys, values, ids, gates)
+
+
+def columns_of(d_exp, d_row, index, block):
+    _, row, _, side = place()
+    return pl.multiple_of((((row ^ d_row) * 2 + index) * 2 + (side ^ d_exp)) * block, block)
+
+
+def projection_kernel(chips, *refs):
+    pieces, (near_weight, far_weight, residual), outs = refs[:4], refs[4:7], refs[7:-2]
+    near, far = refs[-2:]
+    _, _, core, side = place()
+    rows = pieces[0].shape[0]
+    block = outs[0].shape[1] // 2
+    spots = [pl.ds(pl.multiple_of((side ^ d) * rows, rows), rows) for d in range(2)]
+    for d in range(2):
+        near[spots[d], :] = pieces[d][...]
+        far[spots[d], :] = pieces[2 + d][...]
+    for chip, (d_exp, d_row) in enumerate(chips):
+        for index in range(2):
+            start = columns_of(d_exp, d_row, index, block)
+            where = pl.ds(start, block)
+            part = nn_dot(near[...], near_weight[:, where]) + nn_dot(far[...], far_weight[:, where])
+            here = slice(index * block, (index + 1) * block)
+            if chip:
+                outs[chip][:, here] = part.astype(BF16)
+                continue
+            for half in range(2):
+                own = slice(half * rows, (half + 1) * rows)
+                at = pl.ds(pl.multiple_of((half * 2 + core) * rows, rows), rows)
+                outs[0][own, here] = part[own] + residual[at, where].astype(F32)
+
+
+def mixed_kernel(count, *refs):
+    own, others, gain, mixed, sent = refs[0], refs[1:count], refs[count], refs[-2], refs[-1]
+    block = own.shape[1] // 2
+    for index in range(2):
+        here = slice(index * block, (index + 1) * block)
+        total = own[:, here]
+        for other in others:
+            total = total + other[:, here].astype(F32)
+        mixed[:, here] = total
+        scale = gain[:, pl.ds(columns_of(0, 0, index, block), block)]
+        sent[:, here] = (total * scale).astype(BF16)
+
+
+def share_of(slots, slot, group):
+    expert = slots[slot]
+    copies = jnp.int32(0)
+    rank = jnp.int32(0)
+    for index in range(slots.shape[0]):
+        same = (slots[index] == expert).astype(jnp.int32)
+        copies = copies + same
+        rank = rank + jnp.where(index < slot, same, 0)
+    return expert, (lax.rem(group, copies) == rank).astype(F32)
+
+
+def expert_kernel(chips, groups, *refs):
+    slots, gain = refs[0], refs[1]
+    weights = refs[2:6]
+    shares = refs[6 : 6 + len(groups)]
+    parts = refs[6 + len(groups) : -1]
+    act_ref = refs[-1]
+    req, row, core, side = place()
+    rows, width = parts[0].shape
+    block = width // 2
+    hidden, d_model = weights[0].shape
+    gates = None
+    squares = None
+    for chip, (d_exp, d_row) in enumerate(chips):
+        for index in range(2):
+            where = pl.ds(columns_of(d_exp, d_row, index, block), block)
+            here = slice(index * block, (index + 1) * block)
+            part = jnp.concatenate(
+                [parts[group * len(chips) + chip][:, here] for group in range(len(groups))], axis=0
+            )
+            weight = jnp.concatenate([ref[:, where] for ref in weights], axis=0)
+            product = nt_dot(part, weight)
+            plain = part.astype(F32) / gain[:, where]
+            square = jnp.sum(plain * plain, axis=1, keepdims=True)
+            gates = product if gates is None else gates + product
+            squares = square if squares is None else squares + square
+    scale = lax.rsqrt(squares / d_model + 1e-06)
+    gate = gates[:, : 2 * hidden] * scale
+    up = gates[:, 2 * hidden :] * scale
+    act = gate / (1.0 + jnp.exp(-gate)) * up
+    n_tokens = shares[0].shape[1]
+    n_experts = shares[0].shape[0]
+    quarter = rows // 2
+    local = lax.broadcasted_iota(jnp.int32, (rows, 1), 0)
+    token = local + jnp.where(local >= quarter, quarter, 0) + core * quarter
+    lane = lax.broadcasted_iota(jnp.int32, (rows, n_tokens), 1)
+    chosen = (lane == token).astype(F32)
+    expert_lane = lax.broadcasted_iota(jnp.int32, (rows, n_experts), 1)
+    n_kvh = lax.axis_size("kvh")
+    own_slot = req * n_kvh + row * 2 + core
+    other_slot = req * n_kvh + row * 2 + (1 - core)
+    factors = []
+    for group, d_req in enumerate(groups):
+        table = nt_dot(chosen, shares[group][...], precision=lax.Precision.HIGHEST)
+        pair = []
+        for slot in (own_slot, other_slot):
+            expert, serves = share_of(slots, slot, req ^ d_req)
+            share = jnp.sum(jnp.where(expert_lane == expert, table, 0.0), axis=1, keepdims=True)
+            pair.append(share * serves)
+        factors.append(pair)
+    first = jnp.concatenate([pair[0] for pair in factors], axis=0)
+    second = jnp.concatenate([pair[1] for pair in factors], axis=0)
+    unit = lax.broadcasted_iota(jnp.int32, act.shape, 1)
+    act_ref[...] = (act * jnp.where(unit < hidden, first, second)).astype(BF16)
+
+
+def pieces_kernel(chips, weight, *outs):
+    block = outs[0].shape[1] // 2
+    for out, (d_exp, d_row) in zip(outs, chips, strict=True):
+        for index in range(2):
+            where = pl.ds(columns_of(d_exp, d_row, index, block), block)
+            out[:, index * block : (index + 1) * block] = weight[:, where]
+
+
+def combine_kernel(count, groups, *refs):
+    acts, near, far = refs[:count], refs[count : 2 * count], refs[2 * count : 3 * count]
+    rest = refs[3 * count :]
+    mixed = None
+    if groups[0] == 0:
+        mixed, rest = rest[0], rest[1:]
+    _, _, core, _ = place()
+    rows = acts[0].shape[0] // len(groups)
+    total = None
+    for act, low, high in zip(acts, near, far, strict=True):
+        product = nn_dot(act[...], jnp.concatenate([low[...], high[...]], axis=0))
+        total = product if total is None else total + product
+    block = total.shape[1] // 2
+    for index, d_req in enumerate(groups):
+        part = total[index * rows : (index + 1) * rows]
+        if d_req == 0:
+            part = part + mixed[...]
+        own = jnp.where(core == 0, part[:, :block], part[:, block:])
+        other = jnp.where(core == 0, part[:, block:], part[:, :block])
+        rest[2 * index][...] = own.astype(rest[2 * index].dtype)
+        rest[2 * index + 1][...] = other.astype(rest[2 * index + 1].dtype)
+
+
+def final_kernel(count, *refs):
+    own, other, out = refs[:count], refs[count : 2 * count], refs[-1]
+    _, _, core, _ = place()
+    rows = own[0].shape[0] // 2
+    for terms, place_of in ((own, core), (other, 1 - core)):
+        total = terms[0][...]
+        for term in terms[1:]:
+            total = total + term[...].astype(F32)
+        for half in range(2):
+            at = pl.ds(pl.multiple_of((half * 2 + place_of) * rows, rows), rows)
+            out[at, :] = total[half * rows : (half + 1) * rows].astype(BF16)
+
+
+def dense_shards(
+    queries,
+    keys,
+    values,
+    lengths,
+    out_weight,
+    residual,
+    norm_gain,
+    expert_ids,
+    gate_weights,
+    replica_map,
+    w_gate,
+    w_up,
+    w_down,
+):
+    n_req, n_kvh, n_exp = (lax.axis_size(axis) for axis in AXES)
+    d_model = out_weight.shape[1]
+    block = d_model // (n_kvh * n_exp)
+    rows = queries.shape[0]
+    n_experts = expert_ids.shape[1]
+    hidden = w_gate.shape[2]
+    chips = [(d_exp, d_row) for d_row in range(n_kvh // 2) for d_exp in range(n_exp)]
+    n_chips = len(chips)
+    gain = norm_gain.reshape(1, d_model)
+
+    out_weight_far = moved(out_weight, 0, 1, 0)
+    *blocks, shares = attention(
+        queries, keys, values, lengths, expert_ids.T, gate_weights.T, n_experts
+    )
+    blocks[1] = moved(blocks[1], 0, 0, 1)
+    blocks[2] = moved(blocks[2], 0, 1, 0)
+    blocks[3] = moved(blocks[3], 0, 1, 1)
+    down = called(
+        lambda *refs: pieces_kernel(chips, *refs),
+        (w_down[0],),
+        [like((hidden, 2 * block), BF16)] * n_chips,
+        flops=0,
+        name="pieces",
+    )
+    w_in = [w_gate[0].T, w_up[0].T]
+    w_in = [w_in[0], moved(w_in[0], 0, 1, 0), w_in[1], moved(w_in[1], 0, 1, 0)]
+    wide = (rows, 2 * block)
+    sums = called(
+        lambda *refs: projection_kernel(chips, *refs),
+        (*blocks, out_weight, out_weight_far, residual),
+        [like(wide, F32)] + [like(wide, BF16)] * (n_chips - 1),
+        flops=4 * rows * out_weight.size,
+        scratch=[pltpu.VMEM((rows, blocks[0].shape[1]), BF16)] * 2,
+        name="projection",
+    )
+    sums = [
+        sums[chip] if chip == 0 else moved(sums[chip], 0, 2 * d_row, d_exp)
+        for chip, (d_exp, d_row) in enumerate(chips)
+    ]
+    down = [
+        down[chip] if chip == 0 else moved(down[chip], 0, 2 * d_row, d_exp)
+        for chip, (d_exp, d_row) in enumerate(chips)
+    ]
+    down_far = [moved(piece, 0, 1, 0) for piece in down]
+    mixed, sent = called(
+        lambda *refs: mixed_kernel(n_chips, *refs),
+        (*sums, gain),
+        [like(wide, F32), like(wide, BF16)],
+        flops=8 * rows * block,
+        name="mixed",
+    )
+    by_group = [sent if d_req == 0 else moved(sent, d_req, 0, 0) for d_req in range(n_req)]
+    shares = [shares if d_req == 0 else moved(shares, d_req, 0, 0) for d_req in range(n_req)]
+    half = n_req // 2
+    near_terms, far_terms = [], []
+    for groups in (range(half), range(half, n_req)):
+        groups = tuple(groups)
+        parts = [
+            by_group[d_req] if not (d_exp or d_row) else moved(by_group[d_req], 0, 2 * d_row, d_exp)
+            for d_req in groups
+            for d_exp, d_row in chips
+        ]
+        (act,) = called(
+            lambda *refs, groups=groups: expert_kernel(chips, groups, *refs),
+            (replica_map, gain, *w_in, *(shares[d_req] for d_req in groups), *parts),
+            [like((half * rows, 2 * hidden), BF16)],
+            flops=8 * half * rows * d_model * hidden,
+            n_smem=1,
+            name="experts",
+        )
+        acts = [
+            act if not (d_exp or d_row) else moved(act, 0, 2 * d_row, d_exp)
+            for d_exp, d_row in chips
+        ]
+        tail = (mixed,) if groups[0] == 0 else ()
+        terms = called(
+            lambda *refs, groups=groups: combine_kernel(n_chips, groups, *refs),
+            (*acts, *down, *down_far, *tail),
+            [
+                like((rows, block), F32 if d_req == 0 else BF16)
+                for d_req in groups
+                for _ in range(2)
+            ],
+            flops=8 * half * rows * hidden * n_chips * block,
+            name="combine",
+        )
+        for index, d_req in enumerate(groups):
+            near, far = terms[2 * index], terms[2 * index + 1]
+            near_terms.append(near if d_req == 0 else moved(near, d_req, 0, 0))
+            far_terms.append(moved(far, d_req, 1, 0))
+    (out,) = called(
+        lambda *refs: final_kernel(n_req, *refs),
+        (*near_terms, *far_terms),
+        [like((2 * rows, block), BF16)],
+        flops=4 * n_req * rows * block,
+        name="final",
+    )
+    return out
+
+
 def solution(mesh):
     in_specs = (
         P(("req", "exp"), "kvh"),
@@ -187,4 +620,10 @@
         P(("req", "kvh"), "exp", None),
     )
     out_specs = P("req", ("kvh", "exp"))
+    sizes = tuple(mesh.shape[axis] for axis in ("req", "kvh", "exp"))
+
+    def shards(*args):
+        run = dense_shards if is_dense(sizes, args) else routed_shards
+        return run(*args)
+
     return jax.shard_map(shards, mesh=mesh, in_specs=in_specs, out_specs=out_specs, check_vma=False)

time: 305 us -> 100 us (0.33)
  waiting for transfers between devices: 152 us -> 18.6 us
  blocking collectives: 55.6 us -> 0 us
  local copies, waits for them, and re-layouts: 56 us -> 3.27 us
  starting transfers between devices: 5.44 us -> 51.6 us
  Pallas kernels: 0 us -> 26.1 us
  between operations: 13.5 us -> 0.38 us
  matrix products: 12 us -> 0 us
  other arithmetic: 9.29 us -> 0 us
    unnamed x4 -> x0, waiting for transfers between devices: 61.2 us -> none
    ppermute x1 -> x47, starting transfers between devices: 0.79 us -> 51.6 us  [moved(): return lax.ppermute(value, AXES, pairs)]
    reduce_scatter x2 -> x0, waiting for transfers between devices: 45.4 us -> none  [the longest x1 27.1 us: shards(): lax.psum_scatter(lax.dot_general(out_weight, own_heads, (((0,), (1,)), ((...]
    all_to_all x1 -> x0, blocking collectives: 30.6 us -> none  [shards(): lax.all_to_all(jnp.where(source[:, None] >= 0, taken, jnp.zeros((), jnp.b...]
    pallas_call x0 -> x9, Pallas kernels: none -> 26.1 us  [the longest x8 21.7 us: called(): pl.pallas_call(kernel, out_shape=tuple(outs), in_specs=[in_smem()] * n_sm...]
    all_to_all x1 -> x0, waiting for transfers between devices: 25.5 us -> none  [run(): return lax.all_to_all(back, 'req', split_axis=0, concat_axis=0, tiled=True)]
    psum x1 -> x0, blocking collectives: 13.3 us -> none  [shards(): squares = lax.psum(jnp.sum(mixed * mixed, axis=1), ('kvh', 'exp'))]
    slice x2 -> x0, local copies, waits for them, and re-layouts: 12.7 us -> none  [the longest x1 12.5 us: shards(): gathered[:, entry].astype(f32)]
  transfers between devices with their start and end apart: 5 -> 47, of which waited for: 5 -> 13; matrix products, arithmetic and copies ran while one was open for 4% -> 0% of each run, Pallas kernels for 0% -> 24%
where the time goes in v1:
time: 100 us; the launch traced here: 99.9 us
  starting transfers between devices  51.6 us (52%)
  Pallas kernels  26.1 us (26%)
  waiting for transfers between devices  18.6 us (19%)
  local copies, waits for them, and re-layouts  3.27 us (3%)
    ppermute x47, starting transfers between devices, moved(): return lax.ppermute(value, AXES, pairs)  51.6 us
    pallas_call x8, Pallas kernels, called(): pl.pallas_call(kernel, out_shape=tuple(outs), in_specs=[in_smem()] * n_sm...  21.7 us
    ppermute x47, waiting for transfers between devices, moved(): return lax.ppermute(value, AXES, pairs)  18.6 us
    pallas_call x1, Pallas kernels, attention(): pl.pallas_call(attention_kernel, grid=(steps,), out_shape=tuple(outs), in...  4.37 us
    unnamed x94, local copies, waits for them, and re-layouts  3.27 us
  transfers between devices with their start and end apart: 47, of which 13 were waited for; matrix products, arithmetic and copies ran while one was open for 0% of the time, Pallas kernels for 24%

profile of v1, /device:TPU:0, one launch (start us, length us, event | category | flops | bytes accessed | tf_op | source)
XLA Modules:
  0.0 99.9 jit_solution(1129338806249110324)
XLA Ops:
  1.0 4.4 %attention.1 = (bf16[32,256]{1,0:T(8,128)(2,1)}, bf16[32,256]{1,0:T(8,128)(2,1)}, bf16[32,256]{1,0:T(8,128)(2,1)}, bf16[32,256]{1,0:T(8,128)(2,1)}, f32[8,128]{1,0:T(8,128)}) custom-call(s32[128]{0:T(128)} %lengths.1, bf16[64,512]{1,0:T(8,128)(2,1)} %query.1, bf16[64,1,64,128]{3,2,1,0:T(8,128)(2,1)} %key.1, bf16[64,1,64,128]{3,2,1,0:T(8,128)(2,1)} %value.1, ...), custom_call_target="tpu_custom_call" | custom-call | flops 201326592 | bytes 2097152 | tf_op jit(solution)/shard_map/attention/pallas_call | solution.py:316
  5.4 2.5 %collective-permute-start.3 = (bf16[32,256]{1,0:T(8,128)(2,1)}, bf16[32,256]{1,0:T(8,128)(2,1)S(1)}, u32[]{:S(2)}, u32[]{:S(2)}) collective-permute-start(bf16[32,256]{1,0:T(8,128)(2,1)} %get-tuple-element.30), channel_id=1, source_target_pairs={{0,1},{1,0},{2,3},{3,2},{4,5},{5,4},{6,7},{7,6},{8,9},{9,8},{10,11... | collective-permute-start | bytes 49160 | tf_op jit(solution)/shard_map/ppermute | solution.py:206
  7.9 1.6 %collective-permute-start.2 = (f32[8,128]{1,0:T(8,128)}, f32[8,128]{1,0:T(8,128)S(1)}, u32[]{:S(2)}, u32[]{:S(2)}) collective-permute-start(f32[8,128]{1,0:T(8,128)} %get-tuple-element.28.refs_6_), channel_id=1, source_target_pairs={{0,8},{1,9},{2,10},{3,11},{4,12},{5,13},{6,14},{7,15},{8,0},{9,1},... | collective-permute-start | bytes 12296 | tf_op jit(solution)/shard_map/ppermute | solution.py:206
  9.5 2.2 %collective-permute-done.2.refs_7_ = f32[8,128]{1,0:T(8,128)S(1)} collective-permute-done((f32[8,128]{1,0:T(8,128)}, f32[8,128]{1,0:T(8,128)S(1)}, u32[]{:S(2)}, u32[]{:S(2)}) %collective-permute-start.2) | collective-permute-done | bytes 4128 | tf_op jit(solution)/shard_map/ppermute | solution.py:206
  11.7 2.6 %collective-permute-start.28 = (f32[8,128]{1,0:T(8,128)}, f32[8,128]{1,0:T(8,128)S(1)}, u32[]{:S(2)}, u32[]{:S(2)}) collective-permute-start(f32[8,128]{1,0:T(8,128)} %get-tuple-element.28.refs_6_), channel_id=1, source_target_pairs={{0,16},{1,17},{2,18},{3,19},{4,20},{5,21},{6,22},{7,23},{8,24},{9,... | collective-permute-start | bytes 12296 | tf_op jit(solution)/shard_map/ppermute | solution.py:206
  14.3 2.1 %collective-permute-done.28.refs_6_ = f32[8,128]{1,0:T(8,128)S(1)} collective-permute-done((f32[8,128]{1,0:T(8,128)}, f32[8,128]{1,0:T(8,128)S(1)}, u32[]{:S(2)}, u32[]{:S(2)}) %collective-permute-start.28) | collective-permute-done | bytes 4128 | tf_op jit(solution)/shard_map/ppermute | solution.py:206
  16.8 2.1 %pieces.1 = (bf16[192,512]{1,0:T(8,128)(2,1)}, bf16[192,512]{1,0:T(8,128)(2,1)}, bf16[192,512]{1,0:T(8,128)(2,1)}, bf16[192,512]{1,0:T(8,128)(2,1)}) custom-call(bf16[192,2048]{1,0:T(8,128)(2,1)} %bitcast.16), custom_call_target="tpu_custom_call" | custom-call | bytes 1572864 | tf_op jit(solution)/shard_map/pieces/pallas_call | solution.py:234
  19.0 1.9 %collective-permute-start.20 = (bf16[192,512]{1,0:T(8,128)(2,1)}, bf16[192,512]{1,0:T(8,128)(2,1)S(1)}, u32[]{:S(2)}, u32[]{:S(2)}) collective-permute-start(bf16[192,512]{1,0:T(8,128)(2,1)} %get-tuple-element.39), channel_id=1, source_target_pairs={{0,1},{1,0},{2,3},{3,2},{4,5},{5,4},{6,7},{7,6},{8,9},{9,8},{10,11... | collective-permute-start | bytes 589832 | tf_op jit(solution)/shard_map/ppermute | solution.py:206
  20.9 1.5 %collective-permute-start.21 = (bf16[192,512]{1,0:T(8,128)(2,1)}, bf16[192,512]{1,0:T(8,128)(2,1)S(1)}, u32[]{:S(2)}, u32[]{:S(2)}) collective-permute-start(bf16[192,512]{1,0:T(8,128)(2,1)} %get-tuple-element.40), channel_id=1, source_target_pairs={{0,4},{1,5},{2,6},{3,7},{4,0},{5,1},{6,2},{7,3},{8,12},{9,13},{10,... | collective-permute-start | bytes 589832 | tf_op jit(solution)/shard_map/ppermute | solution.py:206
  22.4 3.7 %collective-permute-start.29 = (f32[8,128]{1,0:T(8,128)S(1)}, f32[8,128]{1,0:T(8,128)S(1)}, u32[]{:S(2)}, u32[]{:S(2)}) collective-permute-start(f32[8,128]{1,0:T(8,128)S(1)} %copy-done.41), channel_id=1, source_target_pairs={{0,24},{1,25},{2,26},{3,27},{4,28},{5,29},{6,30},{7,31},{8,16},{9,... | collective-permute-start | bytes 12296 | tf_op jit(solution)/shard_map/ppermute | solution.py:206
  26.1 2.9 %projection.1 = (f32[64,512]{1,0:T(8,128)}, bf16[64,512]{1,0:T(8,128)(2,1)}, bf16[64,512]{1,0:T(8,128)(2,1)}, bf16[64,512]{1,0:T(8,128)(2,1)}) custom-call(bf16[32,256]{1,0:T(8,128)(2,1)} %get-tuple-element.29.refs_0_, bf16[32,256]{1,0:T(8,128)(2,1)} %copy-done.37, bf16[32,256]{1,0:T(8,128)(2,1)} %copy-done.38, bf16[32,256]{1,0:T(8,128)(2,1)} %copy-done.39, ...), custom_call_target="tpu_custom_call" | custom-call | flops 134217728 | bytes 3014656 | tf_op jit(solution)/shard_map/projection/pallas_call | solution.py:234
  29.0 0.6 collective-permute-start.7
  30.2 2.4 %collective-permute-start.9 = (bf16[64,512]{1,0:T(8,128)(2,1)}, bf16[64,512]{1,0:T(8,128)(2,1)S(1)}, u32[]{:S(2)}, u32[]{:S(2)}) collective-permute-start(bf16[64,512]{1,0:T(8,128)(2,1)} %get-tuple-element.36), channel_id=1, source_target_pairs={{0,5},{1,4},{2,7},{3,6},{4,1},{5,0},{6,3},{7,2},{8,13},{9,12},{10,... | collective-permute-start | bytes 196616 | tf_op jit(solution)/shard_map/ppermute | solution.py:206
  32.6 1.4 %collective-permute-done.7.refs_1_ = bf16[64,512]{1,0:T(8,128)(2,1)S(1)} collective-permute-done((bf16[64,512]{1,0:T(8,128)(2,1)}, bf16[64,512]{1,0:T(8,128)(2,1)S(1)}, u32[]{:S(2)}, u32[]{:S(2)}) %collective-permute-start.7) | collective-permute-done | bytes 65568 | tf_op jit(solution)/shard_map/ppermute | solution.py:206
  34.3 1.6 %collective-permute-done.9.refs_3_ = bf16[64,512]{1,0:T(8,128)(2,1)S(1)} collective-permute-done((bf16[64,512]{1,0:T(8,128)(2,1)}, bf16[64,512]{1,0:T(8,128)(2,1)S(1)}, u32[]{:S(2)}, u32[]{:S(2)}) %collective-permute-start.9) | collective-permute-done | bytes 65568 | tf_op jit(solution)/shard_map/ppermute | solution.py:206
  35.9 0.6 copy-done.30
  36.5 1.7 %mixed.1 = (f32[64,512]{1,0:T(8,128)}, bf16[64,512]{1,0:T(8,128)(2,1)}) custom-call(f32[64,512]{1,0:T(8,128)} %get-tuple-element.33.refs_0_, bf16[64,512]{1,0:T(8,128)(2,1)} %copy-done.28, bf16[64,512]{1,0:T(8,128)(2,1)} %copy-done.29, bf16[64,512]{1,0:T(8,128)(2,1)} %copy-done.30, f32[1,2048]{1,0:T(1,128)} %bitcast.17), custom_call_target="tpu_custom_call" | custom-call | flops 131072 | bytes 532480 | tf_op jit(solution)/shard_map/mixed/pallas_call | solution.py:234
  38.2 2.4 %collective-permute-done.22.refs_7_ = bf16[192,512]{1,0:T(8,128)(2,1)S(1)} collective-permute-done((bf16[192,512]{1,0:T(8,128)(2,1)S(1)}, bf16[192,512]{1,0:T(8,128)(2,1)S(1)}, u32[]{:S(2)}, u32[]{:S(2)}) %collective-permute-start.22) | collective-permute-done | bytes 196640 | tf_op jit(solution)/shard_map/ppermute | solution.py:206
  40.6 1.2 %collective-permute-start.10 = (bf16[64,512]{1,0:T(8,128)(2,1)}, bf16[64,512]{1,0:T(8,128)(2,1)S(1)}, u32[]{:S(2)}, u32[]{:S(2)}) collective-permute-start(bf16[64,512]{1,0:T(8,128)(2,1)} %get-tuple-element.37.refs_8_), channel_id=1, source_target_pairs={{0,1},{1,0},{2,3},{3,2},{4,5},{5,4},{6,7},{7,6},{8,9},{9,8},{10,11... | collective-permute-start | bytes 196616 | tf_op jit(solution)/shard_map/ppermute | solution.py:206
  41.8 2.4 %collective-permute-start.11 = (bf16[64,512]{1,0:T(8,128)(2,1)}, bf16[64,512]{1,0:T(8,128)(2,1)S(1)}, u32[]{:S(2)}, u32[]{:S(2)}) collective-permute-start(bf16[64,512]{1,0:T(8,128)(2,1)} %get-tuple-element.37.refs_8_), channel_id=1, source_target_pairs={{0,4},{1,5},{2,6},{3,7},{4,0},{5,1},{6,2},{7,3},{8,12},{9,13},{10,... | collective-permute-start | bytes 196616 | tf_op jit(solution)/shard_map/ppermute | solution.py:206
  44.3 2.6 %collective-permute-start.30 = (bf16[64,512]{1,0:T(8,128)(2,1)}, bf16[64,512]{1,0:T(8,128)(2,1)S(1)}, u32[]{:S(2)}, u32[]{:S(2)}) collective-permute-start(bf16[64,512]{1,0:T(8,128)(2,1)} %get-tuple-element.37.refs_8_), channel_id=1, source_target_pairs={{0,16},{1,17},{2,18},{3,19},{4,20},{5,21},{6,22},{7,23},{8,24},{9,... | collective-permute-start | bytes 196616 | tf_op jit(solution)/shard_map/ppermute | solution.py:206
  46.8 1.8 %collective-permute-start.34 = (bf16[64,512]{1,0:T(8,128)(2,1)}, bf16[64,512]{1,0:T(8,128)(2,1)S(1)}, u32[]{:S(2)}, u32[]{:S(2)}) collective-permute-start(bf16[64,512]{1,0:T(8,128)(2,1)} %get-tuple-element.37.refs_8_), channel_id=1, source_target_pairs={{0,24},{1,25},{2,26},{3,27},{4,28},{5,29},{6,30},{7,31},{8,16},{9,... | collective-permute-start | bytes 196616 | tf_op jit(solution)/shard_map/ppermute | solution.py:206
  48.7 1.5 %collective-permute-start.14 = (bf16[64,512]{1,0:T(8,128)(2,1)S(1)}, bf16[64,512]{1,0:T(8,128)(2,1)S(1)}, u32[]{:S(2)}, u32[]{:S(2)}) collective-permute-start(bf16[64,512]{1,0:T(8,128)(2,1)S(1)} %collective-permute-done.13.refs_12_), channel_id=1, source_target_pairs={{0,1},{1,0},{2,3},{3,2},{4,5},{5,4},{6,7},{7,6},{8,9},{9,8},{10,11... | collective-permute-start | bytes 196616 | tf_op jit(solution)/shard_map/ppermute | solution.py:206
  50.1 1.9 %collective-permute-start.15 = (bf16[64,512]{1,0:T(8,128)(2,1)S(1)}, bf16[64,512]{1,0:T(8,128)(2,1)}, u32[]{:S(2)}, u32[]{:S(2)}) collective-permute-start(bf16[64,512]{1,0:T(8,128)(2,1)S(1)} %collective-permute-done.13.refs_12_), channel_id=1, source_target_pairs={{0,4},{1,5},{2,6},{3,7},{4,0},{5,1},{6,2},{7,3},{8,12},{9,13},{10,... | collective-permute-start | bytes 196616 | tf_op jit(solution)/shard_map/ppermute | solution.py:206
  52.2 2.4 %collective-permute-start.31 = (bf16[64,512]{1,0:T(8,128)(2,1)S(1)}, bf16[64,512]{1,0:T(8,128)(2,1)S(1)}, u32[]{:S(2)}, u32[]{:S(2)}) collective-permute-start(bf16[64,512]{1,0:T(8,128)(2,1)S(1)} %collective-permute-done.30.refs_8_), channel_id=1, source_target_pairs={{0,1},{1,0},{2,3},{3,2},{4,5},{5,4},{6,7},{7,6},{8,9},{9,8},{10,11... | collective-permute-start | bytes 196616 | tf_op jit(solution)/shard_map/ppermute | solution.py:206
  54.6 1.5 %collective-permute-start.32 = (bf16[64,512]{1,0:T(8,128)(2,1)S(1)}, bf16[64,512]{1,0:T(8,128)(2,1)S(1)}, u32[]{:S(2)}, u32[]{:S(2)}) collective-permute-start(bf16[64,512]{1,0:T(8,128)(2,1)S(1)} %collective-permute-done.30.refs_8_), channel_id=1, source_target_pairs={{0,4},{1,5},{2,6},{3,7},{4,0},{5,1},{6,2},{7,3},{8,12},{9,13},{10,... | collective-permute-start | bytes 196616 | tf_op jit(solution)/shard_map/ppermute | solution.py:206
  56.1 1.9 %collective-permute-done.16.refs_15_ = bf16[64,512]{1,0:T(8,128)(2,1)} collective-permute-done((bf16[64,512]{1,0:T(8,128)(2,1)S(1)}, bf16[64,512]{1,0:T(8,128)(2,1)}, u32[]{:S(2)}, u32[]{:S(2)}) %collective-permute-start.16) | collective-permute-done | bytes 65568 | tf_op jit(solution)/shard_map/ppermute | solution.py:206
  58.0 0.8 collective-permute-start.35
  58.8 1.5 %collective-permute-start.36 = (bf16[64,512]{1,0:T(8,128)(2,1)S(1)}, bf16[64,512]{1,0:T(8,128)(2,1)}, u32[]{:S(2)}, u32[]{:S(2)}) collective-permute-start(bf16[64,512]{1,0:T(8,128)(2,1)S(1)} %collective-permute-done.34.refs_12_), channel_id=1, source_target_pairs={{0,4},{1,5},{2,6},{3,7},{4,0},{5,1},{6,2},{7,3},{8,12},{9,13},{10,... | collective-permute-start | bytes 196616 | tf_op jit(solution)/shard_map/ppermute | solution.py:206
  60.3 1.3 %collective-permute-done.33.refs_11_ = bf16[64,512]{1,0:T(8,128)(2,1)S(1)} collective-permute-done((bf16[64,512]{1,0:T(8,128)(2,1)S(1)}, bf16[64,512]{1,0:T(8,128)(2,1)S(1)}, u32[]{:S(2)}, u32[]{:S(2)}) %collective-permute-start.33) | collective-permute-done | bytes 65568 | tf_op jit(solution)/shard_map/ppermute | solution.py:206
  61.6 0.6 copy-done.26
  62.3 4.0 %experts.2.refs_0_ = bf16[128,384]{1,0:T(8,128)(2,1)} custom-call(s32[16]{0:T(128)} %refs_0_.3, f32[1,2048]{1,0:T(1,128)} %bitcast.18, bf16[192,2048]{1,0:T(8,128)(2,1)} %bitcast.11, bf16[192,2048]{1,0:T(8,128)(2,1)} %copy-done, bf16[192,2048]{1,0:T(8,128)(2,1)} %bitcast.14, bf16[192,2048]{1,0:T(8,128)(2,1)} %copy-done.1, ...), custom_call_target="tpu_custom_call" | custom-call | flops 402653184 | bytes 3784768 | tf_op jit(solution)/shard_map/experts/pallas_call | solution.py:234
  66.3 1.7 %collective-permute-start.17 = (bf16[128,384]{1,0:T(8,128)(2,1)}, bf16[128,384]{1,0:T(8,128)(2,1)S(1)}, u32[]{:S(2)}, u32[]{:S(2)}) collective-permute-start(bf16[128,384]{1,0:T(8,128)(2,1)} %experts.2.refs_0_), channel_id=1, source_target_pairs={{0,1},{1,0},{2,3},{3,2},{4,5},{5,4},{6,7},{7,6},{8,9},{9,8},{10,11... | collective-permute-start | bytes 294920 | tf_op jit(solution)/shard_map/ppermute | solution.py:206
  68.0 1.8 %collective-permute-start.18 = (bf16[128,384]{1,0:T(8,128)(2,1)}, bf16[128,384]{1,0:T(8,128)(2,1)S(1)}, u32[]{:S(2)}, u32[]{:S(2)}) collective-permute-start(bf16[128,384]{1,0:T(8,128)(2,1)} %experts.2.refs_0_), channel_id=1, source_target_pairs={{0,4},{1,5},{2,6},{3,7},{4,0},{5,1},{6,2},{7,3},{8,12},{9,13},{10,... | collective-permute-start | bytes 294920 | tf_op jit(solution)/shard_map/ppermute | solution.py:206
  69.9 4.0 %experts.3.refs_0_ = bf16[128,384]{1,0:T(8,128)(2,1)} custom-call(s32[16]{0:T(128)} %refs_0_.3, f32[1,2048]{1,0:T(1,128)} %bitcast.19, bf16[192,2048]{1,0:T(8,128)(2,1)} %bitcast.12, bf16[192,2048]{1,0:T(8,128)(2,1)} %copy-done, bf16[192,2048]{1,0:T(8,128)(2,1)} %bitcast.15, bf16[192,2048]{1,0:T(8,128)(2,1)} %copy-done.1, f32[8,128]{1,0:T(8,128)} %copy-done.40, ...), custom_call_target="tpu_custom_call" | custom-call | flops 402653184 | bytes 3784768 | tf_op jit(solution)/shard_map/experts/pallas_call | solution.py:234
  73.9 1.7 %collective-permute-start.38 = (bf16[128,384]{1,0:T(8,128)(2,1)}, bf16[128,384]{1,0:T(8,128)(2,1)S(1)}, u32[]{:S(2)}, u32[]{:S(2)}) collective-permute-start(bf16[128,384]{1,0:T(8,128)(2,1)} %experts.3.refs_0_), channel_id=1, source_target_pairs={{0,1},{1,0},{2,3},{3,2},{4,5},{5,4},{6,7},{7,6},{8,9},{9,8},{10,11... | collective-permute-start | bytes 294920 | tf_op jit(solution)/shard_map/ppermute | solution.py:206
  75.6 1.8 %collective-permute-start.39 = (bf16[128,384]{1,0:T(8,128)(2,1)}, bf16[128,384]{1,0:T(8,128)(2,1)S(1)}, u32[]{:S(2)}, u32[]{:S(2)}) collective-permute-start(bf16[128,384]{1,0:T(8,128)(2,1)} %experts.3.refs_0_), channel_id=1, source_target_pairs={{0,4},{1,5},{2,6},{3,7},{4,0},{5,1},{6,2},{7,3},{8,12},{9,13},{10,... | collective-permute-start | bytes 294920 | tf_op jit(solution)/shard_map/ppermute | solution.py:206
  78.2 2.7 %combine.2 = (f32[64,256]{1,0:T(8,128)}, f32[64,256]{1,0:T(8,128)}, bf16[64,256]{1,0:T(8,128)(2,1)}, bf16[64,256]{1,0:T(8,128)(2,1)}) custom-call(bf16[128,384]{1,0:T(8,128)(2,1)} %experts.2.refs_0_, bf16[128,384]{1,0:T(8,128)(2,1)} %copy-done.11, bf16[128,384]{1,0:T(8,128)(2,1)} %copy-done.12, bf16[128,384]{1,0:T(8,128)(2,1)} %copy-done.13, ...), custom_call_target="tpu_custom_call" | custom-call | flops 201326592 | bytes 2293760 | tf_op jit(solution)/shard_map/combine/pallas_call | solution.py:234
  80.9 1.6 %collective-permute-start.27 = (bf16[64,256]{1,0:T(8,128)(2,1)}, bf16[64,256]{1,0:T(8,128)(2,1)S(1)}, u32[]{:S(2)}, u32[]{:S(2)}) collective-permute-start(bf16[64,256]{1,0:T(8,128)(2,1)} %get-tuple-element.44), channel_id=1, source_target_pairs={{0,8},{1,9},{2,10},{3,11},{4,12},{5,13},{6,14},{7,15},{8,0},{9,1},... | collective-permute-start | bytes 98312 | tf_op jit(solution)/shard_map/ppermute | solution.py:206
  82.5 0.7 collective-permute-done.40.refs_3_
  83.2 0.6 copy-done.16
  83.8 2.6 %combine.3 = (bf16[64,256]{1,0:T(8,128)(2,1)}, bf16[64,256]{1,0:T(8,128)(2,1)}, bf16[64,256]{1,0:T(8,128)(2,1)}, bf16[64,256]{1,0:T(8,128)(2,1)}) custom-call(bf16[128,384]{1,0:T(8,128)(2,1)} %experts.3.refs_0_, bf16[128,384]{1,0:T(8,128)(2,1)} %copy-done.14, bf16[128,384]{1,0:T(8,128)(2,1)} %copy-done.15, bf16[128,384]{1,0:T(8,128)(2,1)} %copy-done.16, ...), custom_call_target="tpu_custom_call" | custom-call | flops 201326592 | bytes 2097152 | tf_op jit(solution)/shard_map/combine/pallas_call | solution.py:234
  86.4 1.2 %collective-permute-start.41 = (bf16[64,256]{1,0:T(8,128)(2,1)}, bf16[64,256]{1,0:T(8,128)(2,1)S(1)}, u32[]{:S(2)}, u32[]{:S(2)}) collective-permute-start(bf16[64,256]{1,0:T(8,128)(2,1)} %get-tuple-element.45), channel_id=1, source_target_pairs={{0,16},{1,17},{2,18},{3,19},{4,20},{5,21},{6,22},{7,23},{8,24},{9,... | collective-permute-start | bytes 98312 | tf_op jit(solution)/shard_map/ppermute | solution.py:206
  87.6 1.7 %collective-permute-start.42 = (bf16[64,256]{1,0:T(8,128)(2,1)}, bf16[64,256]{1,0:T(8,128)(2,1)S(1)}, u32[]{:S(2)}, u32[]{:S(2)}) collective-permute-start(bf16[64,256]{1,0:T(8,128)(2,1)} %get-tuple-element.46), channel_id=1, source_target_pairs={{0,24},{1,25},{2,26},{3,27},{4,28},{5,29},{6,30},{7,31},{8,16},{9,... | collective-permute-start | bytes 98312 | tf_op jit(solution)/shard_map/ppermute | solution.py:206
  89.8 1.9 %collective-permute-start.45 = (bf16[64,256]{1,0:T(8,128)(2,1)}, bf16[64,256]{1,0:T(8,128)(2,1)S(1)}, u32[]{:S(2)}, u32[]{:S(2)}) collective-permute-start(bf16[64,256]{1,0:T(8,128)(2,1)} %get-tuple-element.49), channel_id=1, source_target_pairs={{0,18},{1,19},{2,16},{3,17},{4,22},{5,23},{6,20},{7,21},{8,26},{9,... | collective-permute-start | bytes 98312 | tf_op jit(solution)/shard_map/ppermute | solution.py:206
  92.0 1.2 %collective-permute-start.46 = (bf16[64,256]{1,0:T(8,128)(2,1)}, bf16[64,256]{1,0:T(8,128)(2,1)S(1)}, u32[]{:S(2)}, u32[]{:S(2)}) collective-permute-start(bf16[64,256]{1,0:T(8,128)(2,1)} %get-tuple-element.50), channel_id=1, source_target_pairs={{0,26},{1,27},{2,24},{3,25},{4,30},{5,31},{6,28},{7,29},{8,18},{9,... | collective-permute-start | bytes 98312 | tf_op jit(solution)/shard_map/ppermute | solution.py:206
  94.2 3.4 %collective-permute-done.46.refs_7_ = bf16[64,256]{1,0:T(8,128)(2,1)S(1)} collective-permute-done((bf16[64,256]{1,0:T(8,128)(2,1)}, bf16[64,256]{1,0:T(8,128)(2,1)S(1)}, u32[]{:S(2)}, u32[]{:S(2)}) %collective-permute-start.46) | collective-permute-done | bytes 32800 | tf_op jit(solution)/shard_map/ppermute | solution.py:206
  98.3 1.6 %final.1 = bf16[128,256]{1,0:T(8,128)(2,1)} custom-call(f32[64,256]{1,0:T(8,128)} %get-tuple-element.43.refs_0_, bf16[64,256]{1,0:T(8,128)(2,1)} %copy-done.31, bf16[64,256]{1,0:T(8,128)(2,1)} %copy-done.32, bf16[64,256]{1,0:T(8,128)(2,1)} %copy-done.33, f32[64,256]{1,0:T(8,128)} %copy-done.27, bf16[64,256]{1,0:T(8,128)(2,1)} %copy-done.34, ...), custom_call_target="tpu_custom_call" | custom-call | flops 262144 | bytes 393216 | tf_op jit(solution)/shard_map/final/pallas_call | solution.py:234
  (149 shorter events, 5.6 us)
Async XLA Ops:
  0.0 22.4 %collective-permute-start.6 = (bf16[256,2048]{1,0:T(8,128)(2,1)}, bf16[256,2048]{1,0:T(8,128)(2,1)S(1)}, u32[]{:S(2)}, u32[]{:S(2)}) collective-permute-start(bf16[256,2048]{1,0:T(8,128)(2,1)} %refs_4_.1), channel_id=1, source_target_pairs={{0,2},{1,3},{2,0},{3,1},{4,6},{5,7},{6,4},{7,5},{8,10},{9,11},{10,... | collective-permute-start | bytes 3145736 | tf_op jit(solution)/shard_map/ppermute | solution.py:206
  0.5 43.8 %collective-permute-start = (bf16[192,2048]{1,0:T(8,128)(2,1)}, bf16[192,2048]{1,0:T(8,128)(2,1)S(1)}, u32[]{:S(2)}, u32[]{:S(2)}) collective-permute-start(bf16[192,2048]{1,0:T(8,128)(2,1)} %bitcast.10), channel_id=1, source_target_pairs={{0,2},{1,3},{2,0},{3,1},{4,6},{5,7},{6,4},{7,5},{8,10},{9,11},{10,... | collective-permute-start | bytes 2359304 | tf_op jit(solution)/shard_map/ppermute | solution.py:206
  0.5 43.7 %collective-permute-start.1 = (bf16[192,2048]{1,0:T(8,128)(2,1)}, bf16[192,2048]{1,0:T(8,128)(2,1)S(1)}, u32[]{:S(2)}, u32[]{:S(2)}) collective-permute-start(bf16[192,2048]{1,0:T(8,128)(2,1)} %bitcast.13), channel_id=1, source_target_pairs={{0,2},{1,3},{2,0},{3,1},{4,6},{5,7},{6,4},{7,5},{8,10},{9,11},{10,... | collective-permute-start | bytes 2359304 | tf_op jit(solution)/shard_map/ppermute | solution.py:206
  5.4 11.1 %collective-permute-start.3 = (bf16[32,256]{1,0:T(8,128)(2,1)}, bf16[32,256]{1,0:T(8,128)(2,1)S(1)}, u32[]{:S(2)}, u32[]{:S(2)}) collective-permute-start(bf16[32,256]{1,0:T(8,128)(2,1)} %get-tuple-element.30), channel_id=1, source_target_pairs={{0,1},{1,0},{2,3},{3,2},{4,5},{5,4},{6,7},{7,6},{8,9},{9,8},{10,11... | collective-permute-start | bytes 49160 | tf_op jit(solution)/shard_map/ppermute | solution.py:206
  7.9 3.8 %collective-permute-start.2 = (f32[8,128]{1,0:T(8,128)}, f32[8,128]{1,0:T(8,128)S(1)}, u32[]{:S(2)}, u32[]{:S(2)}) collective-permute-start(f32[8,128]{1,0:T(8,128)} %get-tuple-element.28.refs_6_), channel_id=1, source_target_pairs={{0,8},{1,9},{2,10},{3,11},{4,12},{5,13},{6,14},{7,15},{8,0},{9,1},... | collective-permute-start | bytes 12296 | tf_op jit(solution)/shard_map/ppermute | solution.py:206
  11.7 4.7 %collective-permute-start.28 = (f32[8,128]{1,0:T(8,128)}, f32[8,128]{1,0:T(8,128)S(1)}, u32[]{:S(2)}, u32[]{:S(2)}) collective-permute-start(f32[8,128]{1,0:T(8,128)} %get-tuple-element.28.refs_6_), channel_id=1, source_target_pairs={{0,16},{1,17},{2,18},{3,19},{4,20},{5,21},{6,22},{7,23},{8,24},{9,... | collective-permute-start | bytes 12296 | tf_op jit(solution)/shard_map/ppermute | solution.py:206
  16.5 2.5 %collective-permute-start.4 = (bf16[32,256]{1,0:T(8,128)(2,1)}, bf16[32,256]{1,0:T(8,128)(2,1)S(1)}, u32[]{:S(2)}, u32[]{:S(2)}) collective-permute-start(bf16[32,256]{1,0:T(8,128)(2,1)} %get-tuple-element.31), channel_id=1, source_target_pairs={{0,2},{1,3},{2,0},{3,1},{4,6},{5,7},{6,4},{7,5},{8,10},{9,11},{10,... | collective-permute-start | bytes 49160 | tf_op jit(solution)/shard_map/ppermute | solution.py:206
  16.5 4.4 %collective-permute-start.5 = (bf16[32,256]{1,0:T(8,128)(2,1)}, bf16[32,256]{1,0:T(8,128)(2,1)S(1)}, u32[]{:S(2)}, u32[]{:S(2)}) collective-permute-start(bf16[32,256]{1,0:T(8,128)(2,1)} %get-tuple-element.32), channel_id=1, source_target_pairs={{0,3},{1,2},{2,1},{3,0},{4,7},{5,6},{6,5},{7,4},{8,11},{9,10},{10,... | collective-permute-start | bytes 49160 | tf_op jit(solution)/shard_map/ppermute | solution.py:206
  19.0 10.7 %collective-permute-start.20 = (bf16[192,512]{1,0:T(8,128)(2,1)}, bf16[192,512]{1,0:T(8,128)(2,1)S(1)}, u32[]{:S(2)}, u32[]{:S(2)}) collective-permute-start(bf16[192,512]{1,0:T(8,128)(2,1)} %get-tuple-element.39), channel_id=1, source_target_pairs={{0,1},{1,0},{2,3},{3,2},{4,5},{5,4},{6,7},{7,6},{8,9},{9,8},{10,11... | collective-permute-start | bytes 589832 | tf_op jit(solution)/shard_map/ppermute | solution.py:206
  20.9 9.3 %collective-permute-start.21 = (bf16[192,512]{1,0:T(8,128)(2,1)}, bf16[192,512]{1,0:T(8,128)(2,1)S(1)}, u32[]{:S(2)}, u32[]{:S(2)}) collective-permute-start(bf16[192,512]{1,0:T(8,128)(2,1)} %get-tuple-element.40), channel_id=1, source_target_pairs={{0,4},{1,5},{2,6},{3,7},{4,0},{5,1},{6,2},{7,3},{8,12},{9,13},{10,... | collective-permute-start | bytes 589832 | tf_op jit(solution)/shard_map/ppermute | solution.py:206
  22.4 6.6 %collective-permute-start.29 = (f32[8,128]{1,0:T(8,128)S(1)}, f32[8,128]{1,0:T(8,128)S(1)}, u32[]{:S(2)}, u32[]{:S(2)}) collective-permute-start(f32[8,128]{1,0:T(8,128)S(1)} %copy-done.41), channel_id=1, source_target_pairs={{0,24},{1,25},{2,26},{3,27},{4,28},{5,29},{6,30},{7,31},{8,16},{9,... | collective-permute-start | bytes 12296 | tf_op jit(solution)/shard_map/ppermute | solution.py:206
  29.0 5.0 %collective-permute-start.7 = (bf16[64,512]{1,0:T(8,128)(2,1)}, bf16[64,512]{1,0:T(8,128)(2,1)S(1)}, u32[]{:S(2)}, u32[]{:S(2)}) collective-permute-start(bf16[64,512]{1,0:T(8,128)(2,1)} %get-tuple-element.34), channel_id=1, source_target_pairs={{0,1},{1,0},{2,3},{3,2},{4,5},{5,4},{6,7},{7,6},{8,9},{9,8},{10,11... | collective-permute-start | bytes 196616 | tf_op jit(solution)/shard_map/ppermute | solution.py:206
  29.6 36.6 %copy-start.4 = (bf16[192,512]{1,0:T(8,128)(2,1)}, bf16[192,512]{1,0:T(8,128)(2,1)S(1)}, u32[]{:S(2)}) copy-start(bf16[192,512]{1,0:T(8,128)(2,1)S(1)} %collective-permute-done.20.refs_5_) | copy-start | bytes 589828
  29.6 4.6 %collective-permute-start.8 = (bf16[64,512]{1,0:T(8,128)(2,1)}, bf16[64,512]{1,0:T(8,128)(2,1)S(1)}, u32[]{:S(2)}, u32[]{:S(2)}) collective-permute-start(bf16[64,512]{1,0:T(8,128)(2,1)} %get-tuple-element.35), channel_id=1, source_target_pairs={{0,4},{1,5},{2,6},{3,7},{4,0},{5,1},{6,2},{7,3},{8,12},{9,13},{10,... | collective-permute-start | bytes 196616 | tf_op jit(solution)/shard_map/ppermute | solution.py:206
  30.2 5.7 %collective-permute-start.9 = (bf16[64,512]{1,0:T(8,128)(2,1)}, bf16[64,512]{1,0:T(8,128)(2,1)S(1)}, u32[]{:S(2)}, u32[]{:S(2)}) collective-permute-start(bf16[64,512]{1,0:T(8,128)(2,1)} %get-tuple-element.36), channel_id=1, source_target_pairs={{0,5},{1,4},{2,7},{3,6},{4,1},{5,0},{6,3},{7,2},{8,13},{9,12},{10,... | collective-permute-start | bytes 196616 | tf_op jit(solution)/shard_map/ppermute | solution.py:206
  34.0 6.6 %collective-permute-start.22 = (bf16[192,512]{1,0:T(8,128)(2,1)S(1)}, bf16[192,512]{1,0:T(8,128)(2,1)S(1)}, u32[]{:S(2)}, u32[]{:S(2)}) collective-permute-start(bf16[192,512]{1,0:T(8,128)(2,1)S(1)} %copy-done.44), channel_id=1, source_target_pairs={{0,5},{1,4},{2,7},{3,6},{4,1},{5,0},{6,3},{7,2},{8,13},{9,12},{10,... | collective-permute-start | bytes 589832 | tf_op jit(solution)/shard_map/ppermute | solution.py:206
  34.2 7.6 %collective-permute-start.23 = (bf16[192,512]{1,0:T(8,128)(2,1)S(1)}, bf16[192,512]{1,0:T(8,128)(2,1)S(1)}, u32[]{:S(2)}, u32[]{:S(2)}) collective-permute-start(bf16[192,512]{1,0:T(8,128)(2,1)S(1)} %copy-done.3), channel_id=1, source_target_pairs={{0,2},{1,3},{2,0},{3,1},{4,6},{5,7},{6,4},{7,5},{8,10},{9,11},{10,... | collective-permute-start | bytes 589832 | tf_op jit(solution)/shard_map/ppermute | solution.py:206
  35.9 5.9 %collective-permute-start.24 = (bf16[192,512]{1,0:T(8,128)(2,1)S(1)}, bf16[192,512]{1,0:T(8,128)(2,1)S(1)}, u32[]{:S(2)}, u32[]{:S(2)}) collective-permute-start(bf16[192,512]{1,0:T(8,128)(2,1)S(1)} %collective-permute-done.20.refs_5_), channel_id=1, source_target_pairs={{0,2},{1,3},{2,0},{3,1},{4,6},{5,7},{6,4},{7,5},{8,10},{9,11},{10,... | collective-permute-start | bytes 589832 | tf_op jit(solution)/shard_map/ppermute | solution.py:206
  40.6 6.3 %collective-permute-start.10 = (bf16[64,512]{1,0:T(8,128)(2,1)}, bf16[64,512]{1,0:T(8,128)(2,1)S(1)}, u32[]{:S(2)}, u32[]{:S(2)}) collective-permute-start(bf16[64,512]{1,0:T(8,128)(2,1)} %get-tuple-element.37.refs_8_), channel_id=1, source_target_pairs={{0,1},{1,0},{2,3},{3,2},{4,5},{5,4},{6,7},{7,6},{8,9},{9,8},{10,11... | collective-permute-start | bytes 196616 | tf_op jit(solution)/shard_map/ppermute | solution.py:206
  41.8 6.8 %collective-permute-start.13 = (bf16[64,512]{1,0:T(8,128)(2,1)}, bf16[64,512]{1,0:T(8,128)(2,1)S(1)}, u32[]{:S(2)}, u32[]{:S(2)}) collective-permute-start(bf16[64,512]{1,0:T(8,128)(2,1)} %get-tuple-element.37.refs_8_), channel_id=1, source_target_pairs={{0,8},{1,9},{2,10},{3,11},{4,12},{5,13},{6,14},{7,15},{8,0},{9,1},... | collective-permute-start | bytes 196616 | tf_op jit(solution)/shard_map/ppermute | solution.py:206
  41.8 8.3 %collective-permute-start.11 = (bf16[64,512]{1,0:T(8,128)(2,1)}, bf16[64,512]{1,0:T(8,128)(2,1)S(1)}, u32[]{:S(2)}, u32[]{:S(2)}) collective-permute-start(bf16[64,512]{1,0:T(8,128)(2,1)} %get-tuple-element.37.refs_8_), channel_id=1, source_target_pairs={{0,4},{1,5},{2,6},{3,7},{4,0},{5,1},{6,2},{7,3},{8,12},{9,13},{10,... | collective-permute-start | bytes 196616 | tf_op jit(solution)/shard_map/ppermute | solution.py:206
  44.2 7.8 %collective-permute-start.12 = (bf16[64,512]{1,0:T(8,128)(2,1)}, bf16[64,512]{1,0:T(8,128)(2,1)S(1)}, u32[]{:S(2)}, u32[]{:S(2)}) collective-permute-start(bf16[64,512]{1,0:T(8,128)(2,1)} %get-tuple-element.37.refs_8_), channel_id=1, source_target_pairs={{0,5},{1,4},{2,7},{3,6},{4,1},{5,0},{6,3},{7,2},{8,13},{9,12},{10,... | collective-permute-start | bytes 196616 | tf_op jit(solution)/shard_map/ppermute | solution.py:206
  44.3 7.9 %collective-permute-start.30 = (bf16[64,512]{1,0:T(8,128)(2,1)}, bf16[64,512]{1,0:T(8,128)(2,1)S(1)}, u32[]{:S(2)}, u32[]{:S(2)}) collective-permute-start(bf16[64,512]{1,0:T(8,128)(2,1)} %get-tuple-element.37.refs_8_), channel_id=1, source_target_pairs={{0,16},{1,17},{2,18},{3,19},{4,20},{5,21},{6,22},{7,23},{8,24},{9,... | collective-permute-start | bytes 196616 | tf_op jit(solution)/shard_map/ppermute | solution.py:206
  46.8 7.7 %collective-permute-start.34 = (bf16[64,512]{1,0:T(8,128)(2,1)}, bf16[64,512]{1,0:T(8,128)(2,1)S(1)}, u32[]{:S(2)}, u32[]{:S(2)}) collective-permute-start(bf16[64,512]{1,0:T(8,128)(2,1)} %get-tuple-element.37.refs_8_), channel_id=1, source_target_pairs={{0,24},{1,25},{2,26},{3,27},{4,28},{5,29},{6,30},{7,31},{8,16},{9,... | collective-permute-start | bytes 196616 | tf_op jit(solution)/shard_map/ppermute | solution.py:206
  48.7 7.4 %collective-permute-start.14 = (bf16[64,512]{1,0:T(8,128)(2,1)S(1)}, bf16[64,512]{1,0:T(8,128)(2,1)S(1)}, u32[]{:S(2)}, u32[]{:S(2)}) collective-permute-start(bf16[64,512]{1,0:T(8,128)(2,1)S(1)} %collective-permute-done.13.refs_12_), channel_id=1, source_target_pairs={{0,1},{1,0},{2,3},{3,2},{4,5},{5,4},{6,7},{7,6},{8,9},{9,8},{10,11... | collective-permute-start | bytes 196616 | tf_op jit(solution)/shard_map/ppermute | solution.py:206
  50.1 6.0 %collective-permute-start.15 = (bf16[64,512]{1,0:T(8,128)(2,1)S(1)}, bf16[64,512]{1,0:T(8,128)(2,1)}, u32[]{:S(2)}, u32[]{:S(2)}) collective-permute-start(bf16[64,512]{1,0:T(8,128)(2,1)S(1)} %collective-permute-done.13.refs_12_), channel_id=1, source_target_pairs={{0,4},{1,5},{2,6},{3,7},{4,0},{5,1},{6,2},{7,3},{8,12},{9,13},{10,... | collective-permute-start | bytes 196616 | tf_op jit(solution)/shard_map/ppermute | solution.py:206
  52.1 5.9 %collective-permute-start.16 = (bf16[64,512]{1,0:T(8,128)(2,1)S(1)}, bf16[64,512]{1,0:T(8,128)(2,1)}, u32[]{:S(2)}, u32[]{:S(2)}) collective-permute-start(bf16[64,512]{1,0:T(8,128)(2,1)S(1)} %collective-permute-done.13.refs_12_), channel_id=1, source_target_pairs={{0,5},{1,4},{2,7},{3,6},{4,1},{5,0},{6,3},{7,2},{8,13},{9,12},{10,... | collective-permute-start | bytes 196616 | tf_op jit(solution)/shard_map/ppermute | solution.py:206
  52.2 5.8 %collective-permute-start.31 = (bf16[64,512]{1,0:T(8,128)(2,1)S(1)}, bf16[64,512]{1,0:T(8,128)(2,1)S(1)}, u32[]{:S(2)}, u32[]{:S(2)}) collective-permute-start(bf16[64,512]{1,0:T(8,128)(2,1)S(1)} %collective-permute-done.30.refs_8_), channel_id=1, source_target_pairs={{0,1},{1,0},{2,3},{3,2},{4,5},{5,4},{6,7},{7,6},{8,9},{9,8},{10,11... | collective-permute-start | bytes 196616 | tf_op jit(solution)/shard_map/ppermute | solution.py:206
  54.6 4.3 %collective-permute-start.32 = (bf16[64,512]{1,0:T(8,128)(2,1)S(1)}, bf16[64,512]{1,0:T(8,128)(2,1)S(1)}, u32[]{:S(2)}, u32[]{:S(2)}) collective-permute-start(bf16[64,512]{1,0:T(8,128)(2,1)S(1)} %collective-permute-done.30.refs_8_), channel_id=1, source_target_pairs={{0,4},{1,5},{2,6},{3,7},{4,0},{5,1},{6,2},{7,3},{8,12},{9,13},{10,... | collective-permute-start | bytes 196616 | tf_op jit(solution)/shard_map/ppermute | solution.py:206
  56.0 5.5 %collective-permute-start.33 = (bf16[64,512]{1,0:T(8,128)(2,1)S(1)}, bf16[64,512]{1,0:T(8,128)(2,1)S(1)}, u32[]{:S(2)}, u32[]{:S(2)}) collective-permute-start(bf16[64,512]{1,0:T(8,128)(2,1)S(1)} %collective-permute-done.30.refs_8_), channel_id=1, source_target_pairs={{0,5},{1,4},{2,7},{3,6},{4,1},{5,0},{6,3},{7,2},{8,13},{9,12},{10,... | collective-permute-start | bytes 196616 | tf_op jit(solution)/shard_map/ppermute | solution.py:206
  56.1 17.8 %collective-permute-start.25 = (bf16[192,512]{1,0:T(8,128)(2,1)S(1)}, bf16[192,512]{1,0:T(8,128)(2,1)S(1)}, u32[]{:S(2)}, u32[]{:S(2)}) collective-permute-start(bf16[192,512]{1,0:T(8,128)(2,1)S(1)} %collective-permute-done.21.refs_6_), channel_id=1, source_target_pairs={{0,2},{1,3},{2,0},{3,1},{4,6},{5,7},{6,4},{7,5},{8,10},{9,11},{10,... | collective-permute-start | bytes 589832 | tf_op jit(solution)/shard_map/ppermute | solution.py:206
  58.0 17.6 %collective-permute-start.26 = (bf16[192,512]{1,0:T(8,128)(2,1)S(1)}, bf16[192,512]{1,0:T(8,128)(2,1)S(1)}, u32[]{:S(2)}, u32[]{:S(2)}) collective-permute-start(bf16[192,512]{1,0:T(8,128)(2,1)S(1)} %collective-permute-done.22.refs_7_), channel_id=1, source_target_pairs={{0,2},{1,3},{2,0},{3,1},{4,6},{5,7},{6,4},{7,5},{8,10},{9,11},{10,... | collective-permute-start | bytes 589832 | tf_op jit(solution)/shard_map/ppermute | solution.py:206
  58.0 8.3 %collective-permute-start.35 = (bf16[64,512]{1,0:T(8,128)(2,1)S(1)}, bf16[64,512]{1,0:T(8,128)(2,1)}, u32[]{:S(2)}, u32[]{:S(2)}) collective-permute-start(bf16[64,512]{1,0:T(8,128)(2,1)S(1)} %collective-permute-done.34.refs_12_), channel_id=1, source_target_pairs={{0,1},{1,0},{2,3},{3,2},{4,5},{5,4},{6,7},{7,6},{8,9},{9,8},{10,11... | collective-permute-start | bytes 196616 | tf_op jit(solution)/shard_map/ppermute | solution.py:206
  58.8 9.2 %collective-permute-start.36 = (bf16[64,512]{1,0:T(8,128)(2,1)S(1)}, bf16[64,512]{1,0:T(8,128)(2,1)}, u32[]{:S(2)}, u32[]{:S(2)}) collective-permute-start(bf16[64,512]{1,0:T(8,128)(2,1)S(1)} %collective-permute-done.34.refs_12_), channel_id=1, source_target_pairs={{0,4},{1,5},{2,6},{3,7},{4,0},{5,1},{6,2},{7,3},{8,12},{9,13},{10,... | collective-permute-start | bytes 196616 | tf_op jit(solution)/shard_map/ppermute | solution.py:206
  62.2 7.7 %collective-permute-start.37 = (bf16[64,512]{1,0:T(8,128)(2,1)S(1)}, bf16[64,512]{1,0:T(8,128)(2,1)}, u32[]{:S(2)}, u32[]{:S(2)}) collective-permute-start(bf16[64,512]{1,0:T(8,128)(2,1)S(1)} %collective-permute-done.34.refs_12_), channel_id=1, source_target_pairs={{0,5},{1,4},{2,7},{3,6},{4,1},{5,0},{6,3},{7,2},{8,13},{9,12},{10,... | collective-permute-start | bytes 196616 | tf_op jit(solution)/shard_map/ppermute | solution.py:206
  66.3 11.1 %collective-permute-start.17 = (bf16[128,384]{1,0:T(8,128)(2,1)}, bf16[128,384]{1,0:T(8,128)(2,1)S(1)}, u32[]{:S(2)}, u32[]{:S(2)}) collective-permute-start(bf16[128,384]{1,0:T(8,128)(2,1)} %experts.2.refs_0_), channel_id=1, source_target_pairs={{0,1},{1,0},{2,3},{3,2},{4,5},{5,4},{6,7},{7,6},{8,9},{9,8},{10,11... | collective-permute-start | bytes 294920 | tf_op jit(solution)/shard_map/ppermute | solution.py:206
  68.0 9.4 %collective-permute-start.18 = (bf16[128,384]{1,0:T(8,128)(2,1)}, bf16[128,384]{1,0:T(8,128)(2,1)S(1)}, u32[]{:S(2)}, u32[]{:S(2)}) collective-permute-start(bf16[128,384]{1,0:T(8,128)(2,1)} %experts.2.refs_0_), channel_id=1, source_target_pairs={{0,4},{1,5},{2,6},{3,7},{4,0},{5,1},{6,2},{7,3},{8,12},{9,13},{10,... | collective-permute-start | bytes 294920 | tf_op jit(solution)/shard_map/ppermute | solution.py:206
  69.9 7.6 %collective-permute-start.19 = (bf16[128,384]{1,0:T(8,128)(2,1)}, bf16[128,384]{1,0:T(8,128)(2,1)S(1)}, u32[]{:S(2)}, u32[]{:S(2)}) collective-permute-start(bf16[128,384]{1,0:T(8,128)(2,1)} %experts.2.refs_0_), channel_id=1, source_target_pairs={{0,5},{1,4},{2,7},{3,6},{4,1},{5,0},{6,3},{7,2},{8,13},{9,12},{10,... | collective-permute-start | bytes 294920 | tf_op jit(solution)/shard_map/ppermute | solution.py:206
  73.9 8.5 %collective-permute-start.38 = (bf16[128,384]{1,0:T(8,128)(2,1)}, bf16[128,384]{1,0:T(8,128)(2,1)S(1)}, u32[]{:S(2)}, u32[]{:S(2)}) collective-permute-start(bf16[128,384]{1,0:T(8,128)(2,1)} %experts.3.refs_0_), channel_id=1, source_target_pairs={{0,1},{1,0},{2,3},{3,2},{4,5},{5,4},{6,7},{7,6},{8,9},{9,8},{10,11... | collective-permute-start | bytes 294920 | tf_op jit(solution)/shard_map/ppermute | solution.py:206
  75.6 6.9 %collective-permute-start.39 = (bf16[128,384]{1,0:T(8,128)(2,1)}, bf16[128,384]{1,0:T(8,128)(2,1)S(1)}, u32[]{:S(2)}, u32[]{:S(2)}) collective-permute-start(bf16[128,384]{1,0:T(8,128)(2,1)} %experts.3.refs_0_), channel_id=1, source_target_pairs={{0,4},{1,5},{2,6},{3,7},{4,0},{5,1},{6,2},{7,3},{8,12},{9,13},{10,... | collective-permute-start | bytes 294920 | tf_op jit(solution)/shard_map/ppermute | solution.py:206
  77.4 5.7 %collective-permute-start.40 = (bf16[128,384]{1,0:T(8,128)(2,1)}, bf16[128,384]{1,0:T(8,128)(2,1)S(1)}, u32[]{:S(2)}, u32[]{:S(2)}) collective-permute-start(bf16[128,384]{1,0:T(8,128)(2,1)} %experts.3.refs_0_), channel_id=1, source_target_pairs={{0,5},{1,4},{2,7},{3,6},{4,1},{5,0},{6,3},{7,2},{8,13},{9,12},{10,... | collective-permute-start | bytes 294920 | tf_op jit(solution)/shard_map/ppermute | solution.py:206
  80.9 8.9 %collective-permute-start.27 = (bf16[64,256]{1,0:T(8,128)(2,1)}, bf16[64,256]{1,0:T(8,128)(2,1)S(1)}, u32[]{:S(2)}, u32[]{:S(2)}) collective-permute-start(bf16[64,256]{1,0:T(8,128)(2,1)} %get-tuple-element.44), channel_id=1, source_target_pairs={{0,8},{1,9},{2,10},{3,11},{4,12},{5,13},{6,14},{7,15},{8,0},{9,1},... | collective-permute-start | bytes 98312 | tf_op jit(solution)/shard_map/ppermute | solution.py:206
  86.4 5.6 %collective-permute-start.41 = (bf16[64,256]{1,0:T(8,128)(2,1)}, bf16[64,256]{1,0:T(8,128)(2,1)S(1)}, u32[]{:S(2)}, u32[]{:S(2)}) collective-permute-start(bf16[64,256]{1,0:T(8,128)(2,1)} %get-tuple-element.45), channel_id=1, source_target_pairs={{0,16},{1,17},{2,18},{3,19},{4,20},{5,21},{6,22},{7,23},{8,24},{9,... | collective-permute-start | bytes 98312 | tf_op jit(solution)/shard_map/ppermute | solution.py:206
  87.6 10.0 %collective-permute-start.43 = (f32[64,256]{1,0:T(8,128)S(1)}, f32[64,256]{1,0:T(8,128)S(1)}, u32[]{:S(2)}, u32[]{:S(2)}) collective-permute-start(f32[64,256]{1,0:T(8,128)S(1)} %copy-done.45), channel_id=1, source_target_pairs={{0,2},{1,3},{2,0},{3,1},{4,6},{5,7},{6,4},{7,5},{8,10},{9,11},{10,... | collective-permute-start | bytes 196616 | tf_op jit(solution)/shard_map/ppermute | solution.py:206
  87.6 6.2 %collective-permute-start.42 = (bf16[64,256]{1,0:T(8,128)(2,1)}, bf16[64,256]{1,0:T(8,128)(2,1)S(1)}, u32[]{:S(2)}, u32[]{:S(2)}) collective-permute-start(bf16[64,256]{1,0:T(8,128)(2,1)} %get-tuple-element.46), channel_id=1, source_target_pairs={{0,24},{1,25},{2,26},{3,27},{4,28},{5,29},{6,30},{7,31},{8,16},{9,... | collective-permute-start | bytes 98312 | tf_op jit(solution)/shard_map/ppermute | solution.py:206
  89.3 4.5 %collective-permute-start.44 = (bf16[64,256]{1,0:T(8,128)(2,1)S(1)}, bf16[64,256]{1,0:T(8,128)(2,1)S(1)}, u32[]{:S(2)}, u32[]{:S(2)}) collective-permute-start(bf16[64,256]{1,0:T(8,128)(2,1)S(1)} %copy-done.46), channel_id=1, source_target_pairs={{0,10},{1,11},{2,8},{3,9},{4,14},{5,15},{6,12},{7,13},{8,2},{9,3},... | collective-permute-start | bytes 98312 | tf_op jit(solution)/shard_map/ppermute | solution.py:206
  89.8 4.5 %collective-permute-start.45 = (bf16[64,256]{1,0:T(8,128)(2,1)}, bf16[64,256]{1,0:T(8,128)(2,1)S(1)}, u32[]{:S(2)}, u32[]{:S(2)}) collective-permute-start(bf16[64,256]{1,0:T(8,128)(2,1)} %get-tuple-element.49), channel_id=1, source_target_pairs={{0,18},{1,19},{2,16},{3,17},{4,22},{5,23},{6,20},{7,21},{8,26},{9,... | collective-permute-start | bytes 98312 | tf_op jit(solution)/shard_map/ppermute | solution.py:206
  92.0 5.6 %collective-permute-start.46 = (bf16[64,256]{1,0:T(8,128)(2,1)}, bf16[64,256]{1,0:T(8,128)(2,1)S(1)}, u32[]{:S(2)}, u32[]{:S(2)}) collective-permute-start(bf16[64,256]{1,0:T(8,128)(2,1)} %get-tuple-element.50), channel_id=1, source_target_pairs={{0,26},{1,27},{2,24},{3,25},{4,30},{5,31},{6,28},{7,29},{8,18},{9,... | collective-permute-start | bytes 98312 | tf_op jit(solution)/shard_map/ppermute | solution.py:206
  (46 other events, 360.1 us)
